TPU v7x, 8 devices: a whole 2x2x1 slice. The times are simulated.
8 devices in a mesh: dp: 1 (over z), tp: 2 (over y), cp: 4 (over x, core).
Axes of the slice: x: 2, y: 2, z: 1, core: 2. Of those that a mesh axis runs over, the one named last changes fastest.
Arguments:
- tokens: bfloat16 [1024, 2048], P(('dp', 'tp', 'cp'))
- norm_attn: bfloat16 [2, 2048], replicated
- norm_mlp: bfloat16 [2, 2048], replicated
- w_q: bfloat16 [2, 2048, 32, 64], P(None, None, 'tp')
- w_k: bfloat16 [2, 2048, 512], P(None, None, 'tp')
- w_v: bfloat16 [2, 2048, 512], P(None, None, 'tp')
- w_o: bfloat16 [2, 32, 64, 2048], P(None, 'tp')
- w_gate: bfloat16 [2, 2048, 8192], P(None, None, 'tp')
- w_up: bfloat16 [2, 2048, 8192], P(None, None, 'tp')
- w_down: bfloat16 [2, 8192, 2048], P(None, 'tp')
Outputs:
- output: bfloat16 [1024, 2048], P(('dp', 'tp', 'cp'))
All inputs are finite; a program needn't handle non-finite values.
Results may differ from a plain program's by a relative error of at most 0.02.
Values are sent between devices in bfloat16 or wider.
A program may use at most 1 GiB of HBM per device.

v0:
```python
import math
import jax
import jax.numpy as jnp
from jax import lax
from jax.sharding import PartitionSpec as P, NamedSharding


def rms_norm(hidden, gain):
    hidden_f = hidden.astype(jnp.float32)
    inv_rms = lax.rsqrt(jnp.mean(hidden_f * hidden_f, axis=-1, keepdims=True) + 1e-5)
    return (hidden_f * inv_rms * gain.astype(jnp.float32)).astype(jnp.bfloat16)


def rotary(values, positions):
    half_dim = values.shape[-1] // 2
    inv_freq = 500000.0 ** (-(jnp.arange(half_dim, dtype=jnp.float32) * 2.0 / values.shape[-1]))
    angles = positions.astype(jnp.float32)[:, None] * inv_freq[None, :]
    cos_ang = jnp.cos(angles)[:, None, :]
    sin_ang = jnp.sin(angles)[:, None, :]
    first = values[..., :half_dim]
    second = values[..., half_dim:]
    return jnp.concatenate([first * cos_ang - second * sin_ang, second * cos_ang + first * sin_ang], axis=-1)


def seg_positions(dev_ids, rows, dev_total):
    offset = jnp.arange(rows)
    half_len = rows // 2
    seg_idx = jnp.where(offset < half_len, dev_ids[..., None], 2 * dev_total - 1 - dev_ids[..., None])
    return seg_idx * half_len + offset % half_len


def attend(queries, keys_all, values_all, q_pos, k_pos, block_rows):
    rows, kv_loc, group, head_dim = queries.shape
    scale = 1.0 / math.sqrt(head_dim)
    q_blocks = queries.reshape(rows // block_rows, block_rows, kv_loc, group, head_dim)
    pos_blocks = q_pos.reshape(rows // block_rows, block_rows)

    def one_block(block):
        q_blk, pos_blk = block
        scores = jnp.einsum('bkgd,tkd->bkgt', q_blk, keys_all, preferred_element_type=jnp.float32) * scale
        visible = k_pos[None, None, None, :] <= pos_blk[:, None, None, None]
        scores = jnp.where(visible, scores, -jnp.inf)
        weights = jnp.exp(scores - jnp.max(scores, axis=-1, keepdims=True))
        row_sum = jnp.sum(weights, axis=-1, keepdims=True)
        mixed = jnp.einsum('bkgt,tkd->bkgd', weights.astype(jnp.bfloat16), values_all, preferred_element_type=jnp.float32)
        return (mixed / row_sum).astype(jnp.bfloat16)

    return lax.map(one_block, (q_blocks, pos_blocks)).reshape(rows, kv_loc * group, head_dim)


def solution(mesh):
    tp_size = mesh.shape['tp']
    cp_size = mesh.shape['cp']
    dev_total = tp_size * cp_size
    row_spec = P(('dp', 'tp', 'cp'), None)
    gain_spec = P(None, None)
    q_spec = P(None, None, 'tp', None)
    col_spec = P(None, None, 'tp')
    o_spec = P(None, 'tp', None, None)
    down_spec = P(None, 'tp', None)

    def body(tokens, norm_attn, norm_mlp, w_q, w_k, w_v, w_o, w_gate, w_up, w_down):
        rows = tokens.shape[0]
        heads_loc = w_q.shape[2]
        head_dim = w_q.shape[3]
        kv_cols = w_k.shape[2]
        tp_idx = lax.axis_index('tp')
        cp_idx = lax.axis_index('cp')
        tp_devs = jnp.arange(tp_size) * cp_size + cp_idx
        pos_rows = seg_positions(tp_devs, rows, dev_total).reshape(tp_size * rows)
        key_devs = jnp.arange(cp_size)[:, None] + jnp.arange(tp_size)[None, :] * cp_size
        pos_keys = seg_positions(key_devs, rows, dev_total).reshape(dev_total * rows)
        hidden = tokens
        for layer_idx in range(w_q.shape[0]):
            normed = lax.all_gather(rms_norm(hidden, norm_attn[layer_idx]), 'tp', axis=0, tiled=True)
            q_proj = jnp.einsum('rd,dhe->rhe', normed, w_q[layer_idx], preferred_element_type=jnp.float32)
            queries = rotary(q_proj, pos_rows).astype(jnp.bfloat16)
            wk_loc = w_k[layer_idx]
            wv_loc = w_v[layer_idx]
            if kv_cols >= head_dim:
                kv_loc = kv_cols // head_dim
            else:
                kv_total = kv_cols * tp_size // head_dim
                start = (tp_idx * kv_total // tp_size) * head_dim
                wk_loc = lax.dynamic_slice_in_dim(lax.all_gather(wk_loc, 'tp', axis=1, tiled=True), start, head_dim, axis=1)
                wv_loc = lax.dynamic_slice_in_dim(lax.all_gather(wv_loc, 'tp', axis=1, tiled=True), start, head_dim, axis=1)
                kv_loc = 1
            k_proj = jnp.dot(normed, wk_loc, preferred_element_type=jnp.float32)
            keys_loc = rotary(k_proj.reshape(tp_size * rows, kv_loc, head_dim), pos_rows).astype(jnp.bfloat16)
            values_loc = jnp.dot(normed, wv_loc, preferred_element_type=jnp.float32).astype(jnp.bfloat16).reshape(tp_size * rows, kv_loc, head_dim)
            keys_all = lax.all_gather(keys_loc, 'cp', axis=0, tiled=True)
            values_all = lax.all_gather(values_loc, 'cp', axis=0, tiled=True)
            grouped = queries.reshape(tp_size * rows, kv_loc, heads_loc // kv_loc, head_dim)
            mixed = attend(grouped, keys_all, values_all, pos_rows, pos_keys, rows // 2)
            attn_part = jnp.einsum('rhe,hed->rd', mixed, w_o[layer_idx], preferred_element_type=jnp.float32)
            attn_out = lax.psum_scatter(attn_part, 'tp', scatter_dimension=0, tiled=True)
            hidden_mid = (hidden.astype(jnp.float32) + attn_out).astype(jnp.bfloat16)
            normed_mlp = lax.all_gather(rms_norm(hidden_mid, norm_mlp[layer_idx]), 'tp', axis=0, tiled=True)
            gate_pre = jnp.dot(normed_mlp, w_gate[layer_idx], preferred_element_type=jnp.float32)
            up_proj = jnp.dot(normed_mlp, w_up[layer_idx], preferred_element_type=jnp.float32)
            hidden_act = (jax.nn.silu(gate_pre) * up_proj).astype(jnp.bfloat16)
            mlp_part = jnp.dot(hidden_act, w_down[layer_idx], preferred_element_type=jnp.float32)
            mlp_out = lax.psum_scatter(mlp_part, 'tp', scatter_dimension=0, tiled=True)
            hidden = (hidden_mid.astype(jnp.float32) + mlp_out).astype(jnp.bfloat16)
        return hidden

    return jax.shard_map(
        body,
        mesh=mesh,
        in_specs=(row_spec, gain_spec, gain_spec, q_spec, col_spec, col_spec, o_spec, col_spec, col_spec, down_spec),
        out_specs=row_spec,
        check_vma=False,
    )
```

profile of v0, /device:TPU:0, one launch (start us, length us, event | category | flops | bytes accessed | tf_op | source)
XLA Modules:
  0.0 378.3 jit_solution(10056505029996916551)
XLA Ops:
  8.6 2.0 fusion.112
  10.7 2.7 slice_bitcast_fusion
  15.5 6.1 %fusion.140 = (bf16[1,2048,16,64]{1,3,2,0:T(8,128)(2,1)}, bf16[1,2048,16,64]{1,3,2,0:T(8,128)(2,1)}) fusion(bf16[2,2048,16,64]{1,3,2,0:T(8,128)(2,1)} %param.17), kind=kLoop, calls=%fused_computation.159 | loop fusion | bytes 16777216 | tf_op jit(solution)/shard_map/slice | solution.py:76
  21.6 10.3 %all-gather.5.cloned.1.call-done = bf16[256,2048]{1,0:T(8,128)(2,1)} async-done(((bf16[128,2048]{1,0:T(8,128)(2,1)}), bf16[256,2048]{1,0:T(8,128)(2,1)}) %all-gather.5.cloned.1.call-update) | async-done | bytes 1048592 | tf_op jit(solution)/shard_map/all_gather | solution.py:75
  31.9 3.8 %fusion.141 = f32[256,1024]{0,1:S(1)} fusion(bf16[256,2048]{1,0:T(8,128)(2,1)} %all-gather.5.cloned.1.call-done, bf16[2048,1024]{0,1:T(8,128)(2,1)} %bitcast.258), kind=kOutput, calls=%fused_computation.160 | convolution fusion | flops 1073741824 | bytes 6291456
  38.4 2.1 fusion.130
  40.6 9.4 %all_gather.25 = bf16[1024,4,64]{0,2,1:T(8,128)(2,1)S(1)} all-gather(bf16[256,4,64]{0,2,1:T(8,128)(2,1)S(1)} %pad_maximum_fusion.2), channel_id=1, replica_groups=mesh['dp'=1,'tp'=2,'cp'=4] {'cp'}, dimensions={0}, use_global_device_ids=true | all-gather | bytes 655360 | tf_op jit(solution)/shard_map/all_gather | solution.py:91
  50.0 2.1 convolution_convert_fusion.1
  52.0 9.1 %all_gather.26 = bf16[1024,4,64]{0,2,1:T(8,128)(2,1)S(1)} all-gather(bf16[256,4,64]{0,2,1:T(8,128)(2,1)S(1)} %bitcast.265), channel_id=1, replica_groups=mesh['dp'=1,'tp'=2,'cp'=4] {'cp'}, dimensions={0}, use_global_device_ids=true | all-gather | bytes 655360 | tf_op jit(solution)/shard_map/all_gather | solution.py:92
  62.1 12.9 %while.22 = (s32[]{:T(128)}, bf16[4,64,4,4,64]{4,1,3,2,0:T(8,128)(2,1)S(1)}, s32[4,64]{1,0:T(4,128)S(1)}, bf16[4,64,4,4,64]{4,1,3,2,0:T(8,128)(2,1)S(1)}, bf16[1...) while((s32[]{:T(128)}, ...), condition=%wide.region_4.5_spmd.clone, body=%wide.region_1.4_spmd.clone.sunk | while | flops 280167424 | bytes 14456377 | solution.py:48
  76.4 4.8 %fusion.100 = f32[256,2048]{1,0:T(8,128)} fusion(bf16[256,16,64]{0,2,1:T(8,128)(2,1)S(1)} %reshape.293, bf16[2,16,64,2048]{3,2,1,0:T(8,128)(2,1)} %param.20), kind=kOutput, calls=%fused_computation.80 | convolution fusion | flops 1073741824 | bytes 6815744 | tf_op jit(solution)/shard_map/rhe,hed->rd/dot_general | solution.py:95
  81.4 28.8 %reduce-scatter.5.cloned.1.call-done = f32[128,2048]{1,0:T(8,128)} async-done(((f32[256,2048]{1,0:T(8,128)}), f32[128,2048]{1,0:T(8,128)}) %reduce-scatter.5.cloned.1.call-update) | async-done | bytes 1048592 | tf_op jit(solution)/shard_map/reduce_scatter | solution.py:96
  110.2 1.5 fusion.114
  112.9 18.2 %all-gather.7.cloned.1.call-done = bf16[256,2048]{1,0:T(8,128)(2,1)} async-done(((bf16[128,2048]{1,0:T(8,128)(2,1)}), bf16[256,2048]{1,0:T(8,128)(2,1)}) %all-gather.7.cloned.1.call-update) | async-done | bytes 1048592 | tf_op jit(solution)/shard_map/all_gather | solution.py:98
  131.1 12.6 %fusion.74 = f32[256,4096]{1,0:T(8,128)} fusion(bf16[256,2048]{1,0:T(8,128)(2,1)} %all-gather.7.cloned.1.call-done, bf16[2,2048,4096]{2,1,0:T(8,128)(2,1)} %param.21), kind=kOutput, calls=%fused_computation.62 | convolution fusion | flops 4294967296 | bytes 22020096 | tf_op jit(solution)/shard_map/dot_general | solution.py:99
  143.7 16.8 %fusion.70 = f32[256,2048]{1,0:T(8,128)} fusion(bf16[2,4096,2048]{2,1,0:T(8,128)(2,1)} %param.23, bf16[256,2048]{1,0:T(8,128)(2,1)S(1)} %copy-done.5, bf16[2,2048,4096]{2,1,0:T(8,128)(2,1)} %param.22, f32[256,4096]{1,0:T(8,128)} %fusion.74), kind=kOutput, calls=%fused_computation.58 | convolution fusion | flops 8596226048 | bytes 40894464 | tf_op jit(solution)/shard_map/dot_general | solution.py:102
  160.6 29.1 %reduce-scatter.7.cloned.1.call-done = f32[128,2048]{1,0:T(8,128)} async-done(((f32[256,2048]{1,0:T(8,128)}), f32[128,2048]{1,0:T(8,128)}) %reduce-scatter.7.cloned.1.call-update) | async-done | bytes 1048592 | tf_op jit(solution)/shard_map/reduce_scatter | solution.py:103
  192.9 17.7 %all-gather.9.cloned.1.call-done = bf16[256,2048]{1,0:T(8,128)(2,1)} async-done(((bf16[128,2048]{1,0:T(8,128)(2,1)}), bf16[256,2048]{1,0:T(8,128)(2,1)}) %all-gather.9.cloned.1.call-update) | async-done | bytes 1048592 | tf_op jit(solution)/shard_map/all_gather | solution.py:75
  210.6 1.7 fusion.127
  212.4 9.4 %all_gather.29 = bf16[1024,4,64]{0,2,1:T(8,128)(2,1)S(1)} all-gather(bf16[256,4,64]{0,2,1:T(8,128)(2,1)S(1)} %pad_maximum_fusion.3), channel_id=1, replica_groups=mesh['dp'=1,'tp'=2,'cp'=4] {'cp'}, dimensions={0}, use_global_device_ids=true | all-gather | bytes 655360 | tf_op jit(solution)/shard_map/all_gather | solution.py:91
  221.8 3.8 %fusion.142 = f32[256,1024]{0,1:S(1)} fusion(bf16[256,2048]{1,0:T(8,128)(2,1)} %all-gather.9.cloned.1.call-done, bf16[2048,1024]{0,1:T(8,128)(2,1)} %bitcast.257), kind=kOutput, calls=%fused_computation.161 | convolution fusion | flops 1073741824 | bytes 6291456
  228.3 2.1 convolution_convert_fusion
  230.4 9.4 %all_gather.30 = bf16[1024,4,64]{0,2,1:T(8,128)(2,1)} all-gather(bf16[256,4,64]{0,2,1:T(8,128)(2,1)S(1)} %bitcast.266), channel_id=1, replica_groups=mesh['dp'=1,'tp'=2,'cp'=4] {'cp'}, dimensions={0}, use_global_device_ids=true | all-gather | bytes 655360 | tf_op jit(solution)/shard_map/all_gather | solution.py:92
  239.7 1.8 pad_maximum_fusion.1
  241.8 13.0 %while.23 = (s32[]{:T(128)}, bf16[4,64,4,4,64]{4,1,3,2,0:T(8,128)(2,1)S(1)}, s32[4,64]{1,0:T(4,128)S(1)}, bf16[4,64,4,4,64]{4,1,3,2,0:T(8,128)(2,1)S(1)}, bf16[1...) while((s32[]{:T(128)}, ...), condition=%wide.region_12.13_spmd.clone, body=%wide.region_9.12_spmd.clone.sunk | while | flops 280167424 | bytes 16553557 | solution.py:48
  256.2 4.8 %fusion.103 = f32[256,2048]{1,0:T(8,128)} fusion(bf16[256,16,64]{0,2,1:T(8,128)(2,1)S(1)} %reshape.295, bf16[2,16,64,2048]{3,2,1,0:T(8,128)(2,1)} %param.20), kind=kOutput, calls=%fused_computation.81 | convolution fusion | flops 1073741824 | bytes 6815744 | tf_op jit(solution)/shard_map/rhe,hed->rd/dot_general | solution.py:95
  261.0 28.8 %reduce-scatter.9.cloned.1.call-done = f32[128,2048]{1,0:T(8,128)} async-done(((f32[256,2048]{1,0:T(8,128)}), f32[128,2048]{1,0:T(8,128)}) %reduce-scatter.9.cloned.1.call-update) | async-done | bytes 1048592 | tf_op jit(solution)/shard_map/reduce_scatter | solution.py:96
  292.4 18.4 %all-gather.11.cloned.1.call-done = bf16[256,2048]{1,0:T(8,128)(2,1)} async-done(((bf16[128,2048]{1,0:T(8,128)(2,1)}), bf16[256,2048]{1,0:T(8,128)(2,1)}) %all-gather.11.cloned.1.call-update) | async-done | bytes 1048592 | tf_op jit(solution)/shard_map/all_gather | solution.py:98
  310.8 12.6 %fusion.68 = f32[256,4096]{1,0:T(8,128)} fusion(bf16[256,2048]{1,0:T(8,128)(2,1)} %all-gather.11.cloned.1.call-done, bf16[2,2048,4096]{2,1,0:T(8,128)(2,1)} %param.21), kind=kOutput, calls=%fused_computation.56 | convolution fusion | flops 4294967296 | bytes 22020096 | tf_op jit(solution)/shard_map/dot_general | solution.py:99
  323.4 16.8 %fusion.64 = f32[256,2048]{1,0:T(8,128)} fusion(bf16[2,4096,2048]{2,1,0:T(8,128)(2,1)} %param.23, bf16[256,2048]{1,0:T(8,128)(2,1)S(1)} %copy-done.6, bf16[2,2048,4096]{2,1,0:T(8,128)(2,1)} %param.22, f32[256,4096]{1,0:T(8,128)} %fusion.68), kind=kOutput, calls=%fused_computation.52 | convolution fusion | flops 8596226048 | bytes 40894464 | tf_op jit(solution)/shard_map/dot_general | solution.py:102
  340.2 29.2 %reduce-scatter.11.cloned.1.call-done = f32[128,2048]{1,0:T(8,128)} async-done(((f32[256,2048]{1,0:T(8,128)}), f32[128,2048]{1,0:T(8,128)}) %reduce-scatter.11.cloned.1.call-update) | async-done | bytes 1048592 | tf_op jit(solution)/shard_map/reduce_scatter | solution.py:103
  369.4 2.1 fusion.125
  (137 shorter events, 46.3 us)
Async XLA Ops:
  6.5 25.3 %all-gather.5.cloned.1.call-start = ((), (), s32[]{:S(2)}) async-start(), calls=%async_computation.4 | async-start | bytes 1572864 | tf_op jit(solution)/shard_map/all_gather | solution.py:75
  10.6 99.6 %reduce-scatter.5.cloned.1.call-start = ((), (), s32[]{:S(2)}) async-start(), calls=%async_computation.5 | async-start | bytes 3145728 | tf_op jit(solution)/shard_map/reduce_scatter | solution.py:96
  38.4 22.8 %copy-start.1 = (bf16[4,64,4,4,32]{4,1,3,2,0:T(8,128)(2,1)S(1)}, bf16[4,64,4,4,32]{4,1,3,2,0:T(8,128)(2,1)}, u32[]{:S(2)}) copy-start(bf16[4,64,4,4,32]{4,1,3,2,0:T(8,128)(2,1)} %copy.34) | copy-start | bytes 786436
  76.4 5.0 %copy-start.4 = (bf16[2,2048]{1,0:T(2,128)(2,1)S(1)}, bf16[2,2048]{1,0:T(2,128)(2,1)}, u32[]{:S(2)}) copy-start(bf16[2,2048]{1,0:T(2,128)(2,1)} %param.16) | copy-start | bytes 24580
  76.4 33.8 %copy-start = (bf16[128,2048]{1,0:T(8,128)(2,1)S(1)}, bf16[128,2048]{1,0:T(8,128)(2,1)}, u32[]{:S(2)}) copy-start(bf16[128,2048]{1,0:T(8,128)(2,1)} %param.14) | copy-start | bytes 1572868
  81.3 49.8 %all-gather.7.cloned.1.call-start = ((), (), s32[]{:S(2)}) async-start(), calls=%async_computation.6 | async-start | bytes 1572864 | tf_op jit(solution)/shard_map/all_gather | solution.py:98
  112.7 77.0 %reduce-scatter.7.cloned.1.call-start = ((), (), s32[]{:S(2)}) async-start(), calls=%async_computation.7 | async-start | bytes 3145728 | tf_op jit(solution)/shard_map/reduce_scatter | solution.py:103
  131.1 12.7 %copy-start.5 = (bf16[256,2048]{1,0:T(8,128)(2,1)S(1)}, bf16[256,2048]{1,0:T(8,128)(2,1)}, u32[]{:S(2)}) copy-start(bf16[256,2048]{1,0:T(8,128)(2,1)} %all-gather.7.cloned.1.call-done) | copy-start | bytes 3145732
  160.5 31.7 %copy-start.2 = (bf16[256,2048]{0,1:T(8,128)(2,1)S(1)}, bf16[256,2048]{0,1:T(8,128)(2,1)}, u32[]{:S(2)}) copy-start(bf16[256,2048]{0,1:T(8,128)(2,1)} %get-tuple-element.185) | copy-start | bytes 3145732
  160.5 50.1 %all-gather.9.cloned.1.call-start = ((), (), s32[]{:S(2)}) async-start(), calls=%async_computation.8 | async-start | bytes 1572864 | tf_op jit(solution)/shard_map/all_gather | solution.py:75
  192.2 97.7 %reduce-scatter.9.cloned.1.call-start = ((), (), s32[]{:S(2)}) async-start(), calls=%async_computation.9 | async-start | bytes 3145728 | tf_op jit(solution)/shard_map/reduce_scatter | solution.py:96
  242.0 1.9 copy-start.3
  245.2 1.9 copy-start.3
  248.5 1.9 copy-start.3
  251.7 1.9 copy-start.3
  261.0 49.8 %all-gather.11.cloned.1.call-start = ((), (), s32[]{:S(2)}) async-start(), calls=%async_computation.10 | async-start | bytes 1572864 | tf_op jit(solution)/shard_map/all_gather | solution.py:98
  292.4 77.0 %reduce-scatter.11.cloned.1.call-start = ((), (), s32[]{:S(2)}) async-start(), calls=%async_computation.11 | async-start | bytes 3145728 | tf_op jit(solution)/shard_map/reduce_scatter | solution.py:103
  310.8 12.6 %copy-start.6 = (bf16[256,2048]{1,0:T(8,128)(2,1)S(1)}, bf16[256,2048]{1,0:T(8,128)(2,1)}, u32[]{:S(2)}) copy-start(bf16[256,2048]{1,0:T(8,128)(2,1)} %all-gather.11.cloned.1.call-done) | copy-start | bytes 3145732
Sparse Core Ops, SparseCore 0:
  10.7 21.0 all-gather.4
  81.4 28.7 reduce-scatter.4
  112.8 18.2 all-gather.6
  160.7 29.0 reduce-scatter.6
  192.3 18.2 all-gather.8
  261.1 28.7 reduce-scatter.8
  292.5 18.2 all-gather.10
  340.3 29.0 reduce-scatter.10
where the time goes:
time: 379 us; the launch traced here: 378 us
  waiting for transfers between devices  181 us (48%)
  matrix products  99.4 us (26%)
  blocking collectives  37.3 us (10%)
  other arithmetic  26.9 us (7%)
  local copies, waits for them, and re-layouts  19.5 us (5%)
  between operations  13.8 us (4%)
    reduce_scatter x2, waiting for transfers between devices, body(): mlp_out = lax.psum_scatter(mlp_part, 'tp', scatter_dimension=0, tiled=True)  58.3 us
    reduce_scatter x2, waiting for transfers between devices, body(): lax.psum_scatter(attn_part, 'tp', scatter_dimension=0, tiled=True)  57.7 us
    all_gather x2, waiting for transfers between devices, body(): lax.all_gather(rms_norm(hidden_mid, norm_mlp[layer_idx]), 'tp', axis=0, t...  36.6 us
    dot_general x2, matrix products, body(): jnp.dot(hidden_act, w_down[layer_idx], preferred_element_type=jnp.float32)  33.5 us
    all_gather x2, waiting for transfers between devices, body(): lax.all_gather(rms_norm(hidden, norm_attn[layer_idx]), 'tp', axis=0, tile...  28 us
    dot_general x2, matrix products, body(): jnp.dot(normed_mlp, w_gate[layer_idx], preferred_element_type=jnp.float32)  25.3 us
    all_gather x2, blocking collectives, body(): keys_all = lax.all_gather(keys_loc, 'cp', axis=0, tiled=True)  18.8 us
    all_gather x2, blocking collectives, body(): values_all = lax.all_gather(values_loc, 'cp', axis=0, tiled=True)  18.5 us
  transfers between devices with their start and end apart: 8, of which 8 were waited for; matrix products, arithmetic and copies ran while one was open for 3% of the time, Pallas kernels for 0%

commit v1 on v0

v1 whole, which is shorter than its diff:
```python
import math
import jax
import jax.numpy as jnp
from jax import lax
from jax.sharding import PartitionSpec as P, NamedSharding


def rms_norm(hidden, gain):
    hidden_f = hidden.astype(jnp.float32)
    inv_rms = lax.rsqrt(jnp.mean(hidden_f * hidden_f, axis=-1, keepdims=True) + 1e-5)
    return (hidden_f * inv_rms * gain.astype(jnp.float32)).astype(jnp.bfloat16)


def rotary(values, positions):
    half_dim = values.shape[-1] // 2
    inv_freq = 500000.0 ** (-(jnp.arange(half_dim, dtype=jnp.float32) * 2.0 / values.shape[-1]))
    angles = positions.astype(jnp.float32)[:, None] * inv_freq[None, :]
    cos_ang = jnp.cos(angles)[:, None, :]
    sin_ang = jnp.sin(angles)[:, None, :]
    first = values[..., :half_dim]
    second = values[..., half_dim:]
    return jnp.concatenate([first * cos_ang - second * sin_ang, second * cos_ang + first * sin_ang], axis=-1)


def seg_positions(dev_ids, rows, dev_total):
    offset = jnp.arange(rows)
    half_len = rows // 2
    seg_idx = jnp.where(offset < half_len, dev_ids[..., None], 2 * dev_total - 1 - dev_ids[..., None])
    return seg_idx * half_len + offset % half_len


def attend(queries, keys_all, values_all, q_pos, k_pos, block_rows):
    rows, kv_loc, group, head_dim = queries.shape
    scale = 1.0 / math.sqrt(head_dim)
    q_blocks = queries.reshape(rows // block_rows, block_rows, kv_loc, group, head_dim)
    pos_blocks = q_pos.reshape(rows // block_rows, block_rows)

    def one_block(block):
        q_blk, pos_blk = block
        scores = jnp.einsum('bkgd,tkd->bkgt', q_blk, keys_all, preferred_element_type=jnp.float32) * scale
        visible = k_pos[None, None, None, :] <= pos_blk[:, None, None, None]
        scores = jnp.where(visible, scores, -jnp.inf)
        weights = jnp.exp(scores - jnp.max(scores, axis=-1, keepdims=True))
        row_sum = jnp.sum(weights, axis=-1, keepdims=True)
        mixed = jnp.einsum('bkgt,tkd->bkgd', weights.astype(jnp.bfloat16), values_all, preferred_element_type=jnp.float32)
        return (mixed / row_sum).astype(jnp.bfloat16)

    return lax.map(one_block, (q_blocks, pos_blocks)).reshape(rows, kv_loc * group, head_dim)


def solution(mesh):
    tp_size = mesh.shape['tp']
    cp_size = mesh.shape['cp']
    dev_total = tp_size * cp_size
    row_spec = P(('dp', 'tp', 'cp'), None)
    gain_spec = P(None, None)
    q_spec = P(None, None, 'tp', None)
    col_spec = P(None, None, 'tp')
    o_spec = P(None, 'tp', None, None)
    down_spec = P(None, 'tp', None)

    swap = [(i, (i + 1) % tp_size) for i in range(tp_size)]

    def body(tokens, norm_attn, norm_mlp, w_q, w_k, w_v, w_o, w_gate, w_up, w_down):
        rows = tokens.shape[0]
        heads_loc = w_q.shape[2]
        head_dim = w_q.shape[3]
        kv_loc = w_k.shape[2] // head_dim
        tp_idx = lax.axis_index('tp')
        cp_idx = lax.axis_index('cp')
        tp_devs = jnp.stack([tp_idx, 1 - tp_idx]) * cp_size + cp_idx
        pos_rows = seg_positions(tp_devs, rows, dev_total).reshape(tp_size * rows)
        hops = (cp_idx - jnp.arange(cp_size)) % cp_size
        key_devs = hops[:, None] + jnp.stack([tp_idx, 1 - tp_idx])[None, :] * cp_size
        pos_keys = seg_positions(key_devs, rows, dev_total).reshape(dev_total * rows)

        def ring(block):
            parts = [block]
            for hop in range(1, cp_size):
                parts.append(lax.ppermute(block, 'cp', [(i, (i + hop) % cp_size) for i in range(cp_size)]))
            return jnp.concatenate(parts, axis=0)

        hidden = tokens
        layers = w_q.shape[0]
        wq_flat = jnp.transpose(w_q, (0, 2, 3, 1)).reshape(layers, heads_loc * head_dim, w_q.shape[1])
        for layer_idx in range(layers):
            hidden_par = lax.ppermute(hidden, 'tp', swap)
            gain = norm_attn[layer_idx]
            normed = jnp.concatenate([rms_norm(hidden, gain), rms_norm(hidden_par, gain)], axis=0)
            q_proj = lax.dot_general(normed, wq_flat[layer_idx], (((1,), (1,)), ((), ())), preferred_element_type=jnp.float32)
            queries = rotary(q_proj.reshape(tp_size * rows, heads_loc, head_dim), pos_rows).astype(jnp.bfloat16)
            k_proj = jnp.dot(normed, w_k[layer_idx], preferred_element_type=jnp.float32)
            keys_loc = rotary(k_proj.reshape(tp_size * rows, kv_loc, head_dim), pos_rows).astype(jnp.bfloat16)
            values_loc = jnp.dot(normed, w_v[layer_idx], preferred_element_type=jnp.float32).astype(jnp.bfloat16)
            kv = ring(jnp.concatenate([keys_loc.reshape(tp_size * rows, kv_loc * head_dim), values_loc], axis=1))
            keys_all = kv[:, :kv_loc * head_dim].reshape(dev_total * rows, kv_loc, head_dim)
            values_all = kv[:, kv_loc * head_dim:].reshape(dev_total * rows, kv_loc, head_dim)
            grouped = queries.reshape(tp_size * rows, kv_loc, heads_loc // kv_loc, head_dim)
            mixed = attend(grouped, keys_all, values_all, pos_rows, pos_keys, rows).reshape(tp_size * rows, heads_loc * head_dim)
            wo = w_o[layer_idx].reshape(heads_loc * head_dim, w_o.shape[3])
            part_par = jnp.dot(mixed[rows:], wo, preferred_element_type=jnp.float32)
            got = lax.ppermute(part_par, 'tp', swap)
            part_own = jnp.dot(mixed[:rows], wo, preferred_element_type=jnp.float32)
            hidden_mid = (hidden.astype(jnp.float32) + (part_own + got)).astype(jnp.bfloat16)
            mid_par = lax.ppermute(hidden_mid, 'tp', swap)
            gain = norm_mlp[layer_idx]

            def mlp_act(rows_in):
                normed_mlp = rms_norm(rows_in, gain)
                gate_pre = jnp.dot(normed_mlp, w_gate[layer_idx], preferred_element_type=jnp.float32)
                up_proj = jnp.dot(normed_mlp, w_up[layer_idx], preferred_element_type=jnp.float32)
                return (jax.nn.silu(gate_pre) * up_proj).astype(jnp.bfloat16)

            act = mlp_act(jnp.concatenate([hidden_mid, mid_par], axis=0))
            down_par = jnp.dot(act[rows:], w_down[layer_idx], preferred_element_type=jnp.float32)
            got = lax.ppermute(down_par, 'tp', swap)
            down_own = jnp.dot(act[:rows], w_down[layer_idx], preferred_element_type=jnp.float32)
            hidden = (hidden_mid.astype(jnp.float32) + (down_own + got)).astype(jnp.bfloat16)
        return hidden

    return jax.shard_map(
        body,
        mesh=mesh,
        in_specs=(row_spec, gain_spec, gain_spec, q_spec, col_spec, col_spec, o_spec, col_spec, col_spec, down_spec),
        out_specs=row_spec,
        check_vma=False,
    )
```

time: 379 us -> 288 us (0.76)
  waiting for transfers between devices: 181 us -> 141 us
  blocking collectives: 37.3 us -> 0 us
  starting transfers between devices: 0.48 us -> 20 us
  between operations: 13.8 us -> 0.47 us
  other arithmetic: 26.9 us -> 14.6 us
  local copies, waits for them, and re-layouts: 19.5 us -> 11.6 us
    ppermute x0 -> x14, waiting for transfers between devices: none -> 141 us  [the longest x2 47.9 us: body(): got = lax.ppermute(part_par, 'tp', swap)]
    reduce_scatter x4 -> x0, waiting for transfers between devices: 116 us -> none  [the longest x2 58.3 us: body(): mlp_out = lax.psum_scatter(mlp_part, 'tp', scatter_dimension=0, tiled=True)]
    all_gather x4 -> x0, waiting for transfers between devices: 64.5 us -> none  [the longest x2 36.6 us: body(): lax.all_gather(rms_norm(hidden_mid, norm_mlp[layer_idx]), 'tp', axis=0, t...]
    all_gather x4 -> x0, blocking collectives: 37.3 us -> none  [the longest x2 18.8 us: body(): keys_all = lax.all_gather(keys_loc, 'cp', axis=0, tiled=True)]
    ppermute x0 -> x14, starting transfers between devices: none -> 20 us  [the longest x6 6.04 us: ring(): lax.ppermute(block, 'cp', [(i, (i + hop) % cp_size) for i in range(cp_siz...]
    dot_general x10 -> x18, matrix products: 76.3 us -> 84.7 us  [the longest x2 17.6 us: mlp_act(): jnp.dot(normed_mlp, w_up[layer_idx], preferred_element_type=jnp.float32)]
    unnamed x2 -> x0, matrix products: 7.6 us -> none
    concatenate x8, local copies, waits for them, and re-layouts: 5.02 us -> 0.43 us  [rotary(): jnp.concatenate([first * cos_ang - second * sin_ang, second * cos_ang + f...]
  transfers between devices with their start and end apart: 8 -> 14, of which waited for: 8 -> 13; matrix products, arithmetic and copies ran while one was open for 3% -> 7% of each run, Pallas kernels for 0% -> 0%
where the time goes in v1:
time: 288 us
  waiting for transfers between devices  141 us (49%)
  matrix products  99.8 us (35%)
  starting transfers between devices  20 us (7%)
  other arithmetic  14.6 us (5%)
  local copies, waits for them, and re-layouts  11.6 us (4%)
    ppermute x2, waiting for transfers between devices, body(): got = lax.ppermute(part_par, 'tp', swap)  47.9 us
    ppermute x2, waiting for transfers between devices, body(): got = lax.ppermute(down_par, 'tp', swap)  44.5 us
    ppermute x2, waiting for transfers between devices, body(): mid_par = lax.ppermute(hidden_mid, 'tp', swap)  23.7 us
    dot_general x2, matrix products, mlp_act(): jnp.dot(normed_mlp, w_up[layer_idx], preferred_element_type=jnp.float32)  17.6 us
    dot_general x2, matrix products, body(): jnp.dot(act[:rows], w_down[layer_idx], preferred_element_type=jnp.float32)  17.5 us
    dot_general x2, matrix products, mlp_act(): jnp.dot(normed_mlp, w_gate[layer_idx], preferred_element_type=jnp.float32)  16.4 us
    ppermute x6, waiting for transfers between devices, ring(): lax.ppermute(block, 'cp', [(i, (i + hop) % cp_size) for i in range(cp_siz...  14.4 us
    dot_general x2, matrix products, body(): jnp.dot(act[rows:], w_down[layer_idx], preferred_element_type=jnp.float32)  14.2 us
  transfers between devices with their start and end apart: 14, of which 13 were waited for; matrix products, arithmetic and copies ran while one was open for 7% of the time, Pallas kernels for 0%

profile of v1, /device:TPU:0, one launch (start us, length us, event | category | flops | bytes accessed | tf_op | source)
XLA Modules:
  0.0 288.1 jit_solution(1917134796410041360)
XLA Ops:
  0.0 3.4 %collective-permute-start = (bf16[128,2048]{1,0:T(8,128)(2,1)}, bf16[128,2048]{1,0:T(8,128)(2,1)S(1)}, u32[]{:S(2)}, u32[]{:S(2)}) collective-permute-start(bf16[128,2048]{1,0:T(8,128)(2,1)} %param.14), channel_id=1, source_target_pairs={{0,4},{4,0},{1,5},{5,1},{2,6},{6,2},{3,7},{7,3}} | collective-permute-start | bytes 1572872 | tf_op jit(solution)/shard_map/ppermute | solution.py:87
  6.3 6.1 %fusion.155 = (bf16[1,16,64,2048]{3,2,1,0:T(8,128)(2,1)}, bf16[1,16,64,2048]{3,2,1,0:T(8,128)(2,1)}) fusion(bf16[2,16,64,2048]{3,2,1,0:T(8,128)(2,1)} %param.20), kind=kLoop, calls=%fused_computation.194 | loop fusion | bytes 16777216 | tf_op jit(solution)/shard_map/slice | solution.py:100
  21.4 3.5 %fusion.101 = f32[256,16,64]{0,2,1:T(8,128)S(1)} fusion(bf16[2,16,64,2048]{3,2,1,0:T(8,128)(2,1)} %bitcast.283, bf16[128,2048]{1,0:T(8,128)(2,1)S(1)} %get-tuple-element.209, bf16[128,2048]{1,0:T(8,128)(2,1)S(1)} %get-tuple-element.208), kind=kOutput, calls=%fused_computation.83 | convolution fusion | flops 1075838976 | bytes 6291456 | tf_op jit(solution)/shard_map/dot_general | solution.py:90
  27.4 4.2 %collective-permute-done.3 = bf16[256,512]{0,1:T(8,128)(2,1)} collective-permute-done((bf16[256,512]{0,1:T(8,128)(2,1)S(1)}, bf16[256,512]{0,1:T(8,128)(2,1)}, u32[]{:S(2)}, u32[]{:S(2)}) %collective-permute-start.3) | collective-permute-done | bytes 262176 | tf_op jit(solution)/shard_map/ppermute | solution.py:80
  33.8 12.4 %while.22 = (s32[]{:T(128)}, bf16[2,128,4,4,64]{1,4,3,2,0:T(8,128)(2,1)S(1)}, s32[2,128]{1,0:T(2,128)S(1)}, bf16[2,128,4,4,64]{1,4,3,2,0:T(8,128)(2,1)S(1)}, bf1...) while((s32[]{:T(128)}, ...), condition=%wide.region_5.6_spmd.clone, body=%wide.region_2.5_spmd.clone.sunk | while | flops 560331776 | bytes 29411668 | solution.py:48
  35.5 2.1 fusion.185
  37.7 2.3 fusion.186
  43.9 2.3 fusion.186
  46.2 3.1 %fusion.160 = f32[128,2048]{1,0:T(8,128)S(1)} fusion(bf16[128,1024]{0,1:T(8,128)(2,1)S(1)} %bitcast.272, bf16[1024,2048]{1,0:T(8,128)(2,1)} %bitcast.261), kind=kOutput, calls=%fused_computation.199 | convolution fusion | flops 536870912 | bytes 5505024 | tf_op jit(solution)/shard_map/dot_general | solution.py:101
  50.9 24.2 %collective-permute-done.4 = f32[128,2048]{1,0:T(8,128)S(1)} collective-permute-done((f32[128,2048]{1,0:T(8,128)S(1)}, f32[128,2048]{1,0:T(8,128)S(1)}, u32[]{:S(2)}, u32[]{:S(2)}) %collective-permute-start.4) | collective-permute-done | bytes 1048608 | tf_op jit(solution)/shard_map/ppermute | solution.py:102
  77.6 12.0 %collective-permute-done.5 = bf16[128,2048]{1,0:T(8,128)(2,1)S(1)} collective-permute-done((bf16[128,2048]{1,0:T(8,128)(2,1)S(1)}, bf16[128,2048]{1,0:T(8,128)(2,1)S(1)}, u32[]{:S(2)}, u32[]{:S(2)}) %collective-permute-start.5) | collective-permute-done | bytes 524320 | tf_op jit(solution)/shard_map/ppermute | solution.py:105
  89.9 8.2 %fusion.78 = f32[256,4096]{1,0:T(8,128)S(1)} fusion(bf16[2,2048,4096]{2,1,0:T(8,128)(2,1)} %param.21, f32[2048]{0:T(1024)S(1)} %bitcast.281, f32[256]{0:T(256)S(1)} %add_rsqrt_fusion.1, bf16[128,2048]{1,0:T(8,128)(2,1)S(1)} %collective-permute-done.5, bf16[128,2048]{1,0:T(8,128)(2,1)S(1)} %fusion.110), kind=kOutput, calls=%fused_computation.66 | convolution fusion | flops 4298637312 | bytes 22029312 | tf_op jit(solution)/shard_map/dot_general | solution.py:110
  98.1 8.9 %fusion.97 = bf16[256,4096]{1,0:T(8,128)(2,1)S(1)} fusion(bf16[2,2048,4096]{2,1,0:T(8,128)(2,1)} %param.22, f32[256,4096]{1,0:T(8,128)S(1)} %fusion.78, f32[2048]{0:T(1024)S(1)} %bitcast.282, f32[256]{0:T(256)S(1)} %add_rsqrt_fusion.1, bf16[128,2048]{1,0:T(8,128)(2,1)S(1)} %collective-permute-done.5, bf16[128,2048]{1,0:T(8,128)(2,1)S(1)} %fusion.110), kind=kOutput, calls=%fused_computation.79 | convolution fusion | flops 4304928768 | bytes 24126464 | tf_op jit(solution)/shard_map/dot_general | solution.py:111
  107.0 7.1 %fusion.72 = f32[128,2048]{1,0:T(8,128)S(1)} fusion(bf16[2,4096,2048]{2,1,0:T(8,128)(2,1)} %param.23, bf16[256,4096]{1,0:T(8,128)(2,1)S(1)} %fusion.97), kind=kOutput, calls=%fused_computation.60 | convolution fusion | flops 2147483648 | bytes 18874368 | tf_op jit(solution)/shard_map/dot_general | solution.py:115
  115.9 22.5 %collective-permute-done.6 = f32[128,2048]{1,0:T(8,128)S(1)} collective-permute-done((f32[128,2048]{1,0:T(8,128)S(1)}, f32[128,2048]{1,0:T(8,128)S(1)}, u32[]{:S(2)}, u32[]{:S(2)}) %collective-permute-start.6) | collective-permute-done | bytes 1048608 | tf_op jit(solution)/shard_map/ppermute | solution.py:116
  138.3 8.4 %fusion.127 = (f32[128]{0:T(128)S(1)}, bf16[128,2048]{1,0:T(8,128)(2,1)S(1)}) fusion(bf16[128,2048]{1,0:T(8,128)(2,1)S(1)} %fusion.110, f32[128,2048]{1,0:T(8,128)S(1)} %collective-permute-done.6, bf16[2,4096,2048]{2,1,0:T(8,128)(2,1)} %param.23, bf16[256,4096]{1,0:T(8,128)(2,1)S(1)} %fusion.97), kind=kOutput, calls=%fused_computation.121 | convolution fusion | flops 2149318656 | bytes 19923456 | tf_op jit(solution)/shard_map/dot_general | solution.py:117
  149.2 9.7 %collective-permute-done.7 = bf16[128,2048]{1,0:T(8,128)(2,1)S(1)} collective-permute-done((bf16[128,2048]{1,0:T(8,128)(2,1)S(1)}, bf16[128,2048]{1,0:T(8,128)(2,1)S(1)}, u32[]{:S(2)}, u32[]{:S(2)}) %collective-permute-start.7) | collective-permute-done | bytes 524320 | tf_op jit(solution)/shard_map/ppermute | solution.py:87
  162.3 2.3 collective-permute-start.9
  164.6 3.5 %fusion.100 = f32[256,16,64]{0,2,1:T(8,128)S(1)} fusion(bf16[2,16,64,2048]{3,2,1,0:T(8,128)(2,1)} %bitcast.284, bf16[128,2048]{1,0:T(8,128)(2,1)S(1)} %get-tuple-element.205, bf16[128,2048]{1,0:T(8,128)(2,1)S(1)} %get-tuple-element.204), kind=kOutput, calls=%fused_computation.81 | convolution fusion | flops 1075838976 | bytes 6291456 | tf_op jit(solution)/shard_map/dot_general | solution.py:90
  168.5 2.3 collective-permute-done.8
  170.9 5.8 %collective-permute-done.9 = bf16[256,512]{0,1:T(8,128)(2,1)S(1)} collective-permute-done((bf16[256,512]{0,1:T(8,128)(2,1)S(1)}, bf16[256,512]{0,1:T(8,128)(2,1)S(1)}, u32[]{:S(2)}, u32[]{:S(2)}) %collective-permute-start.9) | collective-permute-done | bytes 262176 | tf_op jit(solution)/shard_map/ppermute | solution.py:80
  177.0 12.5 %while.23 = (s32[]{:T(128)}, bf16[2,128,4,4,64]{1,4,3,2,0:T(8,128)(2,1)S(1)}, s32[2,128]{1,0:T(2,128)S(1)}, bf16[2,128,4,4,64]{1,4,3,2,0:T(8,128)(2,1)S(1)}, bf1...) while((s32[]{:T(128)}, ...), condition=%wide.region_12.13_spmd.clone, body=%wide.region_9.12_spmd.clone.sunk | while | flops 560331776 | bytes 27314488 | solution.py:48
  181.1 2.3 fusion.191
  187.3 2.3 fusion.191
  189.6 3.1 %fusion.161 = f32[128,2048]{1,0:T(8,128)S(1)} fusion(bf16[128,1024]{0,1:T(8,128)(2,1)S(1)} %bitcast.271, bf16[1024,2048]{1,0:T(8,128)(2,1)} %bitcast.259), kind=kOutput, calls=%fused_computation.200 | convolution fusion | flops 536870912 | bytes 5505024 | tf_op jit(solution)/shard_map/dot_general | solution.py:101
  194.0 23.8 %collective-permute-done.11 = f32[128,2048]{1,0:T(8,128)S(1)} collective-permute-done((f32[128,2048]{1,0:T(8,128)S(1)}, f32[128,2048]{1,0:T(8,128)S(1)}, u32[]{:S(2)}, u32[]{:S(2)}) %collective-permute-start.11) | collective-permute-done | bytes 1048608 | tf_op jit(solution)/shard_map/ppermute | solution.py:102
  219.7 11.7 %collective-permute-done.12 = bf16[128,2048]{1,0:T(8,128)(2,1)S(1)} collective-permute-done((bf16[128,2048]{1,0:T(8,128)(2,1)S(1)}, bf16[128,2048]{1,0:T(8,128)(2,1)S(1)}, u32[]{:S(2)}, u32[]{:S(2)}) %collective-permute-start.12) | collective-permute-done | bytes 524320 | tf_op jit(solution)/shard_map/ppermute | solution.py:105
  231.7 8.2 %fusion.70 = f32[256,4096]{1,0:T(8,128)S(1)} fusion(bf16[2,2048,4096]{2,1,0:T(8,128)(2,1)} %param.21, f32[2048]{0:T(1024)S(1)} %bitcast.279, f32[256]{0:T(256)S(1)} %add_rsqrt_fusion, bf16[128,2048]{1,0:T(8,128)(2,1)S(1)} %collective-permute-done.12, bf16[128,2048]{1,0:T(8,128)(2,1)S(1)} %fusion.111), kind=kOutput, calls=%fused_computation.58 | convolution fusion | flops 4298637312 | bytes 22029312 | tf_op jit(solution)/shard_map/dot_general | solution.py:110
  239.9 8.7 %fusion.94 = bf16[256,4096]{1,0:T(8,128)(2,1)S(1)} fusion(bf16[2,2048,4096]{2,1,0:T(8,128)(2,1)} %param.22, f32[256,4096]{1,0:T(8,128)S(1)} %fusion.70, f32[2048]{0:T(1024)S(1)} %bitcast.280, f32[256]{0:T(256)S(1)} %add_rsqrt_fusion, bf16[128,2048]{1,0:T(8,128)(2,1)S(1)} %collective-permute-done.12, bf16[128,2048]{1,0:T(8,128)(2,1)S(1)} %fusion.111), kind=kOutput, calls=%fused_computation.78 | convolution fusion | flops 4304928768 | bytes 24126464 | tf_op jit(solution)/shard_map/dot_general | solution.py:111
  248.6 7.1 %fusion.64 = f32[128,2048]{1,0:T(8,128)S(1)} fusion(bf16[2,4096,2048]{2,1,0:T(8,128)(2,1)} %param.23, bf16[256,4096]{1,0:T(8,128)(2,1)S(1)} %fusion.94), kind=kOutput, calls=%fused_computation.52 | convolution fusion | flops 2147483648 | bytes 18874368 | tf_op jit(solution)/shard_map/dot_general | solution.py:115
  257.0 22.0 %collective-permute-done.13 = f32[128,2048]{1,0:T(8,128)S(1)} collective-permute-done((f32[128,2048]{1,0:T(8,128)S(1)}, f32[128,2048]{1,0:T(8,128)S(1)}, u32[]{:S(2)}, u32[]{:S(2)}) %collective-permute-start.13) | collective-permute-done | bytes 1048608 | tf_op jit(solution)/shard_map/ppermute | solution.py:116
  279.0 9.1 %add_convert_fusion = bf16[128,2048]{1,0:T(8,128)(2,1)} fusion(bf16[128,2048]{1,0:T(8,128)(2,1)S(1)} %fusion.111, f32[128,2048]{1,0:T(8,128)S(1)} %collective-permute-done.13, bf16[2,4096,2048]{2,1,0:T(8,128)(2,1)} %param.23, bf16[256,4096]{1,0:T(8,128)(2,1)S(1)} %fusion.94), kind=kOutput, calls=%fused_computation.142 | convolution fusion | flops 2148532224 | bytes 19922944 | tf_op jit(solution)/shard_map/dot_general | solution.py:117
  (109 shorter events, 47.2 us)
Async XLA Ops:
  0.0 15.3 %collective-permute-start = (bf16[128,2048]{1,0:T(8,128)(2,1)}, bf16[128,2048]{1,0:T(8,128)(2,1)S(1)}, u32[]{:S(2)}, u32[]{:S(2)}) collective-permute-start(bf16[128,2048]{1,0:T(8,128)(2,1)} %param.14), channel_id=1, source_target_pairs={{0,4},{4,0},{1,5},{5,1},{2,6},{6,2},{3,7},{7,3}} | collective-permute-start | bytes 1572872 | tf_op jit(solution)/shard_map/ppermute | solution.py:87
  6.3 8.0 %copy-start.4 = (bf16[2,2048]{1,0:T(2,128)(2,1)S(1)}, bf16[2,2048]{1,0:T(2,128)(2,1)}, u32[]{:S(2)}) copy-start(bf16[2,2048]{1,0:T(2,128)(2,1)} %param.15) | copy-start | bytes 24580
  6.3 9.2 %copy-start.2 = (bf16[128,2048]{1,0:T(8,128)(2,1)S(1)}, bf16[128,2048]{1,0:T(8,128)(2,1)}, u32[]{:S(2)}) copy-start(bf16[128,2048]{1,0:T(8,128)(2,1)} %param.14) | copy-start | bytes 1572868
  14.4 3.2 %copy-start.6 = (bf16[2,2048,256]{2,1,0:T(8,128)(2,1)S(1)}, bf16[2,2048,256]{2,1,0:T(8,128)(2,1)}, u32[]{:S(2)}) copy-start(bf16[2,2048,256]{2,1,0:T(8,128)(2,1)} %param.19) | copy-start | bytes 6291460
  18.2 8.0 %collective-permute-start.1 = (bf16[256,512]{0,1:T(8,128)(2,1)S(1)}, bf16[256,512]{0,1:T(8,128)(2,1)S(1)}, u32[]{:S(2)}, u32[]{:S(2)}) collective-permute-start(bf16[256,512]{0,1:T(8,128)(2,1)S(1)} %pad_maximum_fusion.14), channel_id=1, source_target_pairs={{0,1},{1,2},{2,3},{3,0},{4,5},{5,6},{6,7},{7,4}} | collective-permute-start | bytes 786440 | tf_op jit(solution)/shard_map/ppermute | solution.py:80
  18.2 9.2 %collective-permute-start.2 = (bf16[256,512]{0,1:T(8,128)(2,1)S(1)}, bf16[256,512]{0,1:T(8,128)(2,1)}, u32[]{:S(2)}, u32[]{:S(2)}) collective-permute-start(bf16[256,512]{0,1:T(8,128)(2,1)S(1)} %pad_maximum_fusion.14), channel_id=1, source_target_pairs={{0,2},{1,3},{2,0},{3,1},{4,6},{5,7},{6,4},{7,5}} | collective-permute-start | bytes 786440 | tf_op jit(solution)/shard_map/ppermute | solution.py:80
  19.9 11.7 %collective-permute-start.3 = (bf16[256,512]{0,1:T(8,128)(2,1)S(1)}, bf16[256,512]{0,1:T(8,128)(2,1)}, u32[]{:S(2)}, u32[]{:S(2)}) collective-permute-start(bf16[256,512]{0,1:T(8,128)(2,1)S(1)} %pad_maximum_fusion.14), channel_id=1, source_target_pairs={{0,3},{1,0},{2,1},{3,2},{4,7},{5,4},{6,5},{7,6}} | collective-permute-start | bytes 786440 | tf_op jit(solution)/shard_map/ppermute | solution.py:80
  35.5 2.2 copy-start.3
  41.7 2.2 copy-start.3
  46.2 28.9 %copy-start.1 = (bf16[1,16,64,2048]{3,2,1,0:T(8,128)(2,1)S(1)}, bf16[1,16,64,2048]{3,2,1,0:T(8,128)(2,1)}, u32[]{:S(2)}) copy-start(bf16[1,16,64,2048]{3,2,1,0:T(8,128)(2,1)} %get-tuple-element.185) | copy-start | bytes 12582916
  49.3 28.2 %copy-start.5 = (bf16[2,2048]{1,0:T(2,128)(2,1)S(1)}, bf16[2,2048]{1,0:T(2,128)(2,1)}, u32[]{:S(2)}) copy-start(bf16[2,2048]{1,0:T(2,128)(2,1)} %param.16) | copy-start | bytes 24580
  49.3 25.7 %collective-permute-start.4 = (f32[128,2048]{1,0:T(8,128)S(1)}, f32[128,2048]{1,0:T(8,128)S(1)}, u32[]{:S(2)}, u32[]{:S(2)}) collective-permute-start(f32[128,2048]{1,0:T(8,128)S(1)} %fusion.160), channel_id=1, source_target_pairs={{0,4},{4,0},{1,5},{5,1},{2,6},{6,2},{3,7},{7,3}} | collective-permute-start | bytes 3145736 | tf_op jit(solution)/shard_map/ppermute | solution.py:102
  75.8 13.8 %collective-permute-start.5 = (bf16[128,2048]{1,0:T(8,128)(2,1)S(1)}, bf16[128,2048]{1,0:T(8,128)(2,1)S(1)}, u32[]{:S(2)}, u32[]{:S(2)}) collective-permute-start(bf16[128,2048]{1,0:T(8,128)(2,1)S(1)} %fusion.110), channel_id=1, source_target_pairs={{0,4},{4,0},{1,5},{5,1},{2,6},{6,2},{3,7},{7,3}} | collective-permute-start | bytes 1572872 | tf_op jit(solution)/shard_map/ppermute | solution.py:105
  114.1 24.2 %collective-permute-start.6 = (f32[128,2048]{1,0:T(8,128)S(1)}, f32[128,2048]{1,0:T(8,128)S(1)}, u32[]{:S(2)}, u32[]{:S(2)}) collective-permute-start(f32[128,2048]{1,0:T(8,128)S(1)} %fusion.72), channel_id=1, source_target_pairs={{0,4},{4,0},{1,5},{5,1},{2,6},{6,2},{3,7},{7,3}} | collective-permute-start | bytes 3145736 | tf_op jit(solution)/shard_map/ppermute | solution.py:116
  146.8 12.1 %collective-permute-start.7 = (bf16[128,2048]{1,0:T(8,128)(2,1)S(1)}, bf16[128,2048]{1,0:T(8,128)(2,1)S(1)}, u32[]{:S(2)}, u32[]{:S(2)}) collective-permute-start(bf16[128,2048]{1,0:T(8,128)(2,1)S(1)} %get-tuple-element.174), channel_id=1, source_target_pairs={{0,4},{4,0},{1,5},{5,1},{2,6},{6,2},{3,7},{7,3}} | collective-permute-start | bytes 1572872 | tf_op jit(solution)/shard_map/ppermute | solution.py:87
  161.7 6.8 %collective-permute-start.10 = (bf16[256,512]{0,1:T(8,128)(2,1)S(1)}, bf16[256,512]{0,1:T(8,128)(2,1)S(1)}, u32[]{:S(2)}, u32[]{:S(2)}) collective-permute-start(bf16[256,512]{0,1:T(8,128)(2,1)S(1)} %pad_maximum_fusion.15), channel_id=1, source_target_pairs={{0,3},{1,0},{2,1},{3,2},{4,7},{5,4},{6,5},{7,6}} | collective-permute-start | bytes 786440 | tf_op jit(solution)/shard_map/ppermute | solution.py:80
  162.0 8.9 %collective-permute-start.8 = (bf16[256,512]{0,1:T(8,128)(2,1)S(1)}, bf16[256,512]{0,1:T(8,128)(2,1)S(1)}, u32[]{:S(2)}, u32[]{:S(2)}) collective-permute-start(bf16[256,512]{0,1:T(8,128)(2,1)S(1)} %pad_maximum_fusion.15), channel_id=1, source_target_pairs={{0,1},{1,2},{2,3},{3,0},{4,5},{5,6},{6,7},{7,4}} | collective-permute-start | bytes 786440 | tf_op jit(solution)/shard_map/ppermute | solution.py:80
  162.3 14.4 %collective-permute-start.9 = (bf16[256,512]{0,1:T(8,128)(2,1)S(1)}, bf16[256,512]{0,1:T(8,128)(2,1)S(1)}, u32[]{:S(2)}, u32[]{:S(2)}) collective-permute-start(bf16[256,512]{0,1:T(8,128)(2,1)S(1)} %pad_maximum_fusion.15), channel_id=1, source_target_pairs={{0,2},{1,3},{2,0},{3,1},{4,6},{5,7},{6,4},{7,5}} | collective-permute-start | bytes 786440 | tf_op jit(solution)/shard_map/ppermute | solution.py:80
  189.6 28.2 %copy-start = (bf16[1,16,64,2048]{3,2,1,0:T(8,128)(2,1)S(1)}, bf16[1,16,64,2048]{3,2,1,0:T(8,128)(2,1)}, u32[]{:S(2)}) copy-start(bf16[1,16,64,2048]{3,2,1,0:T(8,128)(2,1)} %get-tuple-element.184) | copy-start | bytes 12582916
  192.7 25.0 %collective-permute-start.11 = (f32[128,2048]{1,0:T(8,128)S(1)}, f32[128,2048]{1,0:T(8,128)S(1)}, u32[]{:S(2)}, u32[]{:S(2)}) collective-permute-start(f32[128,2048]{1,0:T(8,128)S(1)} %fusion.161), channel_id=1, source_target_pairs={{0,4},{4,0},{1,5},{5,1},{2,6},{6,2},{3,7},{7,3}} | collective-permute-start | bytes 3145736 | tf_op jit(solution)/shard_map/ppermute | solution.py:102
  218.5 12.9 %collective-permute-start.12 = (bf16[128,2048]{1,0:T(8,128)(2,1)S(1)}, bf16[128,2048]{1,0:T(8,128)(2,1)S(1)}, u32[]{:S(2)}, u32[]{:S(2)}) collective-permute-start(bf16[128,2048]{1,0:T(8,128)(2,1)S(1)} %fusion.111), channel_id=1, source_target_pairs={{0,4},{4,0},{1,5},{5,1},{2,6},{6,2},{3,7},{7,3}} | collective-permute-start | bytes 1572872 | tf_op jit(solution)/shard_map/ppermute | solution.py:105
  255.7 23.3 %collective-permute-start.13 = (f32[128,2048]{1,0:T(8,128)S(1)}, f32[128,2048]{1,0:T(8,128)S(1)}, u32[]{:S(2)}, u32[]{:S(2)}) collective-permute-start(f32[128,2048]{1,0:T(8,128)S(1)} %fusion.64), channel_id=1, source_target_pairs={{0,4},{4,0},{1,5},{5,1},{2,6},{6,2},{3,7},{7,3}} | collective-permute-start | bytes 3145736 | tf_op jit(solution)/shard_map/ppermute | solution.py:116

commit v2 on v0

v2 whole, which is shorter than its diff:
```python
import functools
import math

import jax
import jax.numpy as jnp
from jax import lax
from jax.experimental import pallas as pl
from jax.experimental.pallas import tpu as pltpu
from jax.sharding import PartitionSpec as P

MESH = pl.DeviceIdType.MESH
F32 = jnp.float32
BF16 = jnp.bfloat16
ROWS, SEG, D, HEAD, FF = 128, 64, 2048, 64, 4096
CH, NCH = 256, 8
GCH, NGC = 512, 8
RING = 4
LAYERS = 2
EXP2_SCALE = math.log2(math.e) / math.sqrt(HEAD)


def kernel(tokens, gain_attn, gain_mlp, cos_ref, sin_ref, wq, wk, wv, wo, wg, wu, wd, out,
           x_own, x_par, a_ref, qh, o_ref, kv, act, sbuf, rbuf, slot, wk_v, wv_v, wg_v, wu_v, wd_v,
           tok_sem, out_sem, slot_sem, kvw_sem, gu_sem, wd_sem, xs_sem, xr_sem, ps_sem, pr_sem, ks_sem, kr_sem):
    t = lax.axis_index('tp')
    c = lax.axis_index('cp')
    other = {'tp': 1 - t}

    def load_slot(src):
        return [pltpu.make_async_copy(src.at[pl.ds(i * 512, 512)], slot.at[pl.ds(i * 512, 512)], slot_sem.at[i]) for i in range(2)]

    def load_kvw(l):
        return [pltpu.make_async_copy(wk.at[l], wk_v, kvw_sem.at[0]), pltpu.make_async_copy(wv.at[l], wv_v, kvw_sem.at[1])]

    def load_gu(l, j):
        cols = pl.ds(pl.multiple_of(j * GCH, GCH), GCH)
        return [pltpu.make_async_copy(wg.at[l, :, cols], wg_v.at[j], gu_sem.at[0, j]),
                pltpu.make_async_copy(wu.at[l, :, cols], wu_v.at[j], gu_sem.at[1, j])]

    def load_wd(l, j):
        cols = pl.ds(pl.multiple_of(j * CH, CH), CH)
        s = lax.rem(j, RING)
        return pltpu.make_async_copy(wd.at[l, :, cols], wd_v.at[s], wd_sem.at[s])

    def start(copies):
        for copy in copies:
            copy.start()

    def wait(copies):
        for copy in copies:
            copy.wait()

    def send_x(src, j):
        return pltpu.make_async_remote_copy(src, x_par.at[j], xs_sem.at[j], xr_sem.at[j], other, MESH)

    def send_part(j):
        return pltpu.make_async_remote_copy(sbuf.at[j], rbuf.at[j], ps_sem.at[j], pr_sem.at[j], other, MESH)

    def segments(g, ti, ci):
        k = (ti if g == 0 else 1 - ti) * 4 + ci
        return k, 15 - k

    def send_kv(l, hop, g, i, ci):
        rows = pl.ds(pl.multiple_of(segments(g, t, ci)[i] * SEG, SEG), SEG)
        place = kv.at[l, rows, :]
        return pltpu.make_async_remote_copy(place, place, ks_sem.at[l, hop, g, i], kr_sem.at[l, hop, g, i],
                                            {'cp': lax.rem(c + hop + 1, 4)}, MESH)

    tok = [pltpu.make_async_copy(tokens.at[:, pl.ds(j * CH, CH)], x_own.at[j], tok_sem.at[j]) for j in range(NCH)]
    start(tok)
    start(load_kvw(0))
    start(load_slot(wq.at[0]))

    barrier = pltpu.get_barrier_semaphore()
    pl.semaphore_signal(barrier, inc=1, device_id=other, device_id_type=MESH)
    for hop in range(3):
        pl.semaphore_signal(barrier, inc=1, device_id={'cp': lax.rem(c + hop + 1, 4)}, device_id_type=MESH)
    pl.semaphore_wait(barrier, 4)
    for j in range(NCH):
        send_x(tokens.at[:, pl.ds(j * CH, CH)], j).start()
    for j in range(NGC):
        start(load_gu(0, j))
    for j in range(RING):
        load_wd(0, j).start()

    lane = lax.broadcasted_iota(jnp.int32, (ROWS, 128), 1)
    first_half = (lane % HEAD) < HEAD // 2
    low = lane < HEAD
    low_seg = lax.broadcasted_iota(jnp.int32, (SEG, 128), 1) < HEAD
    diff = (lax.broadcasted_iota(jnp.int32, (4 * SEG, 512), 1)
            - lax.broadcasted_iota(jnp.int32, (4 * SEG, 512), 0) % SEG)

    def norm(x_ref, gain, g):
        total = jnp.zeros((ROWS, 1), F32)
        for j in range(NCH):
            x = x_ref[j].astype(F32)
            total = total + jnp.sum(x * x, axis=-1, keepdims=True)
        inv = lax.rsqrt(total * (1.0 / D) + 1e-5)
        for j in range(NCH):
            cols = pl.ds(j * CH, CH)
            a_ref[g, :, cols] = (x_ref[j].astype(F32) * inv * gain[:, cols]).astype(BF16)

    def rope(v, g):
        swapped = jnp.where(first_half, pltpu.roll(v, 128 - HEAD // 2, 1), pltpu.roll(v, HEAD // 2, 1))
        return v * cos_ref[g] + swapped * sin_ref[g]

    def qkv(l, g):
        k_new = jnp.dot(a_ref[g], wk_v[...], preferred_element_type=F32)
        v_new = jnp.dot(a_ref[g], wv_v[...], preferred_element_type=F32).astype(BF16)
        k_new = jnp.concatenate([rope(k_new[:, :128], g), rope(k_new[:, 128:], g)], axis=1).astype(BF16)
        for i in range(2):
            rows = pl.ds(pl.multiple_of(segments(g, t, c)[i] * SEG, SEG), SEG)
            kv[l, rows, 0:256] = k_new[i * SEG:(i + 1) * SEG]
            kv[l, rows, 256:512] = v_new[i * SEG:(i + 1) * SEG]
        for i in range(2):
            for hop in (1, 0, 2):
                send_kv(l, hop, g, i, c).start()
        for h in range(4):
            q = lax.dot_general(a_ref[g], slot[h * 256:(h + 1) * 256, :], (((1,), (1,)), ((), ())), preferred_element_type=F32)
            for pair in range(2):
                both = rope(q[:, pair * 128:(pair + 1) * 128], g)
                turned = pltpu.roll(both, HEAD, 1)
                for odd in range(2):
                    value = both if odd == h % 2 else turned
                    value = jnp.where(low if h % 2 == 0 else ~low, value, 0.0).astype(BF16)
                    n = pair * 2 + odd
                    for i in range(2):
                        qh[g, i, h, n * SEG:(n + 1) * SEG, :] = value[i * SEG:(i + 1) * SEG]

    def attention(l, g):
        for i in range(2):
            seg = segments(g, t, c)[i]
            free = 512 * i
            visible = diff <= seg * SEG - free
            for parity in range(2):
                def pair_step(p, carry, i=i, free=free, visible=visible, parity=parity):
                    h = 2 * p + parity
                    k_cols = pl.ds(pl.multiple_of(p * 128, 128), 128)
                    v_cols = pl.ds(pl.multiple_of(256 + p * 128, 128), 128)
                    q = qh[g, i, h]
                    nt = (((1,), (1,)), ((), ()))
                    s_end = lax.dot_general(q, kv[l, pl.ds(free, 512), k_cols], nt, preferred_element_type=F32)
                    s_end = jnp.where(visible, s_end, -jnp.inf)
                    top = jnp.max(s_end, axis=-1, keepdims=True)
                    if free:
                        s_free = lax.dot_general(q, kv[l, pl.ds(0, free), k_cols], nt, preferred_element_type=F32)
                        top = jnp.maximum(top, jnp.max(s_free, axis=-1, keepdims=True))
                    e_end = jnp.exp2((s_end - top) * EXP2_SCALE)
                    total = jnp.sum(e_end, axis=-1, keepdims=True)
                    mixed = jnp.dot(e_end.astype(BF16), kv[l, pl.ds(free, 512), v_cols], preferred_element_type=F32)
                    if free:
                        e_free = jnp.exp2((s_free - top) * EXP2_SCALE)
                        total = total + jnp.sum(e_free, axis=-1, keepdims=True)
                        mixed = mixed + jnp.dot(e_free.astype(BF16), kv[l, pl.ds(0, free), v_cols], preferred_element_type=F32)
                    mixed = mixed / total
                    for pair in range(2):
                        sides = []
                        for odd in range(2):
                            n = pair * 2 + odd
                            value = mixed[n * SEG:(n + 1) * SEG]
                            sides.append(value if odd == parity else pltpu.roll(value, HEAD, 1))
                        cols = pl.ds(pl.multiple_of(h * 256 + pair * 128, 128), 128)
                        o_ref[g, i * SEG:(i + 1) * SEG, cols] = jnp.where(low_seg, sides[0], sides[1]).astype(BF16)
                    return carry
                lax.fori_loop(0, 2, pair_step, 0)

    def slot_chunk(lhs, j):
        return jnp.dot(lhs, slot[:, pl.ds(pl.multiple_of(j * CH, CH), CH)], preferred_element_type=F32)

    def reduce_chunk(own, j):
        send_part(j).wait_recv()
        return (x_own[j].astype(F32) + (own + rbuf[j])).astype(BF16)

    for l in range(LAYERS):
        last = l == LAYERS - 1
        if l == 0:
            wait(tok)
        norm(x_own, gain_attn[l], 0)
        wait(load_kvw(l))
        wait(load_slot(wq.at[l]))
        qkv(l, 0)
        for j in range(NCH):
            send_x(x_own.at[j], j).wait_recv()
        norm(x_par, gain_attn[l], 1)
        qkv(l, 1)
        start(load_slot(wo.at[l]))
        if not last:
            start(load_kvw(l + 1))
        for g in range(2):
            for i in range(2):
                for hop in range(3):
                    send_kv(l, hop, g, i, lax.rem(c + 3 - hop, 4)).wait_recv()
        attention(l, 1)
        wait(load_slot(wo.at[l]))

        def o_send(j, carry, l=l):
            part = slot_chunk(o_ref[1], j)
            if l > 0:
                send_part(j).wait_send()
            sbuf[j] = part
            send_part(j).start()
            return carry
        lax.fori_loop(0, NCH, o_send, 0)
        attention(l, 0)

        def o_reduce(j, carry):
            new = reduce_chunk(slot_chunk(o_ref[0], j), j)
            send_x(x_own.at[j], j).wait_send()
            x_own[j] = new
            send_x(x_own.at[j], j).start()
            return carry
        lax.fori_loop(0, NCH, o_reduce, 0)
        if not last:
            start(load_slot(wq.at[l + 1]))

        def gate_up(g, l=l, last=last):
            def step(j, carry):
                if g == 0:
                    wait(load_gu(l, j))
                gate = jnp.dot(a_ref[g], wg_v[j], preferred_element_type=F32)
                up = jnp.dot(a_ref[g], wu_v[j], preferred_element_type=F32)
                act[g, :, pl.ds(pl.multiple_of(j * GCH, GCH), GCH)] = (gate * jax.nn.sigmoid(gate) * up).astype(BF16)
                if g == 1 and not last:
                    start(load_gu(l + 1, j))
                return carry
            lax.fori_loop(0, NGC, step, 0)

        norm(x_own, gain_mlp[l], 0)
        gate_up(0)
        for j in range(NCH):
            send_x(x_own.at[j], j).wait_recv()
        norm(x_par, gain_mlp[l], 1)
        gate_up(1)

        def down_chunk(g, j, l=l):
            load_wd(l, j).wait()
            return jnp.dot(act[g], wd_v[lax.rem(j, RING)], preferred_element_type=F32)

        def down_send(j, carry, l=l):
            part = down_chunk(1, j)
            load_wd(l, lax.rem(j + RING, NCH)).start()
            send_part(j).wait_send()
            sbuf[j] = part
            send_part(j).start()
            return carry
        lax.fori_loop(0, NCH, down_send, 0)

        def down_reduce(j, carry, l=l, last=last):
            own = down_chunk(0, j)
            if last:
                @pl.when(j < NCH - RING)
                def _():
                    load_wd(l, j + RING).start()
            else:
                @pl.when(j < NCH - RING)
                def _():
                    load_wd(l, j + RING).start()

                @pl.when(j >= NCH - RING)
                def _():
                    load_wd(l + 1, j + RING - NCH).start()
            new = reduce_chunk(own, j)
            send_x(x_own.at[j], j).wait_send()
            x_own[j] = new
            cols = pl.ds(pl.multiple_of(j * CH, CH), CH)
            if last:
                pltpu.make_async_copy(x_own.at[j], out.at[:, cols], out_sem.at[j]).start()
            else:
                send_x(x_own.at[j], j).start()
            return carry
        lax.fori_loop(0, NCH, down_reduce, 0)

    for j in range(NCH):
        send_part(j).wait_send()
        pltpu.make_async_copy(x_own.at[j], out.at[:, pl.ds(j * CH, CH)], out_sem.at[j]).wait()
    for l in range(LAYERS):
        for g in range(2):
            for i in range(2):
                for hop in range(3):
                    send_kv(l, hop, g, i, c).wait_send()


def solution(mesh):
    tp_size = mesh.shape['tp']
    cp_size = mesh.shape['cp']
    row_spec = P(('dp', 'tp', 'cp'), None)
    gain_spec = P(None, None)
    q_spec = P(None, None, 'tp', None)
    col_spec = P(None, None, 'tp')
    o_spec = P(None, 'tp', None, None)
    down_spec = P(None, 'tp', None)

    def body(tokens, norm_attn, norm_mlp, w_q, w_k, w_v, w_o, w_gate, w_up, w_down):
        t = lax.axis_index('tp')
        c = lax.axis_index('cp')
        dev = jnp.stack([t, 1 - t]) * cp_size + c
        seg = jnp.stack([dev, 2 * tp_size * cp_size - 1 - dev], axis=1)
        pos = (seg[:, :, None] * SEG + jnp.arange(SEG)[None, None, :]).reshape(2, ROWS)
        inv_freq = 500000.0 ** (-(jnp.arange(HEAD // 2, dtype=F32) * 2.0 / HEAD))
        angles = pos.astype(F32)[:, :, None] * inv_freq
        cos, sin = jnp.cos(angles), jnp.sin(angles)
        cos = jnp.concatenate([cos, cos, cos, cos], axis=-1)
        sin = jnp.concatenate([-sin, sin, -sin, sin], axis=-1)
        wq = jnp.transpose(w_q, (0, 2, 3, 1)).reshape(LAYERS, 1024, D)
        wo = w_o.reshape(LAYERS, 1024, D)
        hbm = pl.BlockSpec(memory_space=pl.ANY)
        vmem = pl.BlockSpec(memory_space=pltpu.VMEM)
        dma = pltpu.SemaphoreType.DMA
        return pl.pallas_call(
            kernel,
            out_shape=jax.ShapeDtypeStruct((ROWS, D), BF16),
            in_specs=[hbm, vmem, vmem, vmem, vmem] + [hbm] * 7,
            out_specs=hbm,
            scratch_shapes=[
                pltpu.VMEM((NCH, ROWS, CH), BF16),
                pltpu.VMEM((NCH, ROWS, CH), BF16),
                pltpu.VMEM((2, ROWS, D), BF16),
                pltpu.VMEM((2, 2, 4, 4 * SEG, 128), BF16),
                pltpu.VMEM((2, ROWS, 1024), BF16),
                pltpu.VMEM((LAYERS, 1024, 512), BF16),
                pltpu.VMEM((2, ROWS, FF), BF16),
                pltpu.VMEM((NCH, ROWS, CH), F32),
                pltpu.VMEM((NCH, ROWS, CH), F32),
                pltpu.VMEM((1024, D), BF16),
                pltpu.VMEM((D, 256), BF16),
                pltpu.VMEM((D, 256), BF16),
                pltpu.VMEM((NGC, D, GCH), BF16),
                pltpu.VMEM((NGC, D, GCH), BF16),
                pltpu.VMEM((RING, FF, CH), BF16),
                dma((NCH,)), dma((NCH,)), dma((2,)), dma((2,)), dma((2, NGC)), dma((RING,)),
                dma((NCH,)), dma((NCH,)), dma((NCH,)), dma((NCH,)),
                dma((LAYERS, 3, 2, 2)), dma((LAYERS, 3, 2, 2)),
            ],
            compiler_params=pltpu.CompilerParams(
                collective_id=0, has_side_effects=True, vmem_limit_bytes=67_000_000),
            name='decoder',
        )(tokens, norm_attn.astype(F32).reshape(LAYERS, 1, D), norm_mlp.astype(F32).reshape(LAYERS, 1, D), cos, sin,
          wq, w_k, w_v, wo, w_gate, w_up, w_down)

    return jax.shard_map(
        body,
        mesh=mesh,
        in_specs=(row_spec, gain_spec, gain_spec, q_spec, col_spec, col_spec, o_spec, col_spec, col_spec, down_spec),
        out_specs=row_spec,
        check_vma=False,
    )
```

time: 379 us -> 196 us (0.52)
  Pallas kernels: 0 us -> 190 us
  waiting for transfers between devices: 181 us -> 0 us
  matrix products: 99.4 us -> 0 us
  blocking collectives: 37.3 us -> 0 us
  other arithmetic: 26.9 us -> 1.6 us
  local copies, waits for them, and re-layouts: 19.5 us -> 4.74 us
  between operations: 13.8 us -> 0.03 us
    pallas_call x0 -> x1, Pallas kernels: none -> 190 us  [body(): pl.pallas_call(kernel, out_shape=jax.ShapeDtypeStruct((ROWS, D), BF16), i...]
    reduce_scatter x4 -> x0, waiting for transfers between devices: 116 us -> none  [the longest x2 58.3 us: body(): mlp_out = lax.psum_scatter(mlp_part, 'tp', scatter_dimension=0, tiled=True)]
    dot_general x26 -> x0, matrix products: 91.8 us -> none  [the longest x2 33.5 us: body(): jnp.dot(hidden_act, w_down[layer_idx], preferred_element_type=jnp.float32)]
    all_gather x4 -> x0, waiting for transfers between devices: 64.5 us -> none  [the longest x2 36.6 us: body(): lax.all_gather(rms_norm(hidden_mid, norm_mlp[layer_idx]), 'tp', axis=0, t...]
    all_gather x4 -> x0, blocking collectives: 37.3 us -> none  [the longest x2 18.8 us: body(): keys_all = lax.all_gather(keys_loc, 'cp', axis=0, tiled=True)]
    reduce_sum x12 -> x0, other arithmetic: 14.2 us -> none  [the longest x8 8.63 us: one_block(): row_sum = jnp.sum(weights, axis=-1, keepdims=True)]
    unnamed x2 -> x0, matrix products: 7.6 us -> none
    convert_element_type x6 -> x1, other arithmetic: 7.19 us -> 0.01 us  [body(): angles = pos.astype(F32)[:, :, None] * inv_freq]
  transfers between devices with their start and end apart: 8 -> 0, of which waited for: 8 -> 0; matrix products, arithmetic and copies ran while one was open for 3% -> 0% of each run, Pallas kernels for 0% -> 0%
where the time goes in v2:
time: 196 us
  Pallas kernels  190 us (97%)
  local copies, waits for them, and re-layouts  4.74 us (2%)
    pallas_call x1, Pallas kernels, body(): pl.pallas_call(kernel, out_shape=jax.ShapeDtypeStruct((ROWS, D), BF16), i...  190 us

profile of v2, /device:TPU:0, one launch (start us, length us, event | category | flops | bytes accessed | tf_op | source)
XLA Modules:
  0.0 196.1 jit_solution(17965007989798317921)
XLA Ops:
  0.0 0.1 add_multiply_fusion.1
  0.1 0.1 add.47
  0.2 0.1 add.48
  0.3 0.1 add.50
  0.4 1.3 reshape.132.gain_attn
  1.7 1.3 reshape.134.gain_mlp
  3.0 0.5 fusion
  3.5 1.0 pad_maximum_fusion
  4.5 189.7 %decoder.1 = bf16[128,2048]{1,0:T(8,128)(2,1)} custom-call(bf16[128,2048]{1,0:T(8,128)(2,1)} %tokens.1, f32[2,1,2048]{2,1,0:T(1,128)} %reshape.132.gain_attn, f32[2,1,2048]{2,1,0:T(1,128)} %reshape.134.gain_mlp, f32[2,128,128]{2,1,0:T(8,128)} %get-tuple-element.10.cos_ref, f32[2,128,128]{2,1,0:T(8,128)} %get-tuple-element.11.sin_ref, ...), custom_call_target="tpu_custom_call" | custom-call | tf_op jit(solution)/shard_map/decoder/pallas_call | solution.py:309
  194.2 1.9 copy.12
  (4 shorter events, 0.0 us)

commit v3 on v2

--- a/solution.py
+++ b/solution.py
@@ -1,8 +1,8 @@
-import functools
 import math
 
 import jax
 import jax.numpy as jnp
+import numpy as np
 from jax import lax
 from jax.experimental import pallas as pl
 from jax.experimental.pallas import tpu as pltpu
@@ -15,16 +15,22 @@
 CH, NCH = 256, 8
 GCH, NGC = 512, 8
 RING = 4
+PIECES, PIECE = 8, 32
+FIRST, MIDDLE, LATE = (0, 1, 2, 3), (4, 5), (6, 7)
 LAYERS = 2
 EXP2_SCALE = math.log2(math.e) / math.sqrt(HEAD)
 
 
-def kernel(tokens, gain_attn, gain_mlp, cos_ref, sin_ref, wq, wk, wv, wo, wg, wu, wd, out,
-           x_own, x_par, a_ref, qh, o_ref, kv, act, sbuf, rbuf, slot, wk_v, wv_v, wg_v, wu_v, wd_v,
-           tok_sem, out_sem, slot_sem, kvw_sem, gu_sem, wd_sem, xs_sem, xr_sem, ps_sem, pr_sem, ks_sem, kr_sem):
+def kernel(tokens, gain_attn, gain_mlp, table, wq, wk, wv, wo, wg, wu, wd, out,
+           x_own, x_par, a_ref, qh, o_ref, o_x, kv, act, sbuf, rbuf, slot, wo_x, wk_v, wv_v, wg_v, wu_v, wd_v,
+           turns, cos_ref, sin_ref,
+           tok_sem, out_sem, slot_sem, kvw_sem, gu_sem, wd_sem, turn_sem, xs_sem, xr_sem, ps_sem, pr_sem, ds_sem, dr_sem,
+           ks_sem, kr_sem, os_sem, or_sem, ws_sem, wr_sem, fs_sem, fr_sem):
     t = lax.axis_index('tp')
     c = lax.axis_index('cp')
     other = {'tp': 1 - t}
+    beside, across, corner = c + 1 - 2 * lax.rem(c, 2), lax.rem(c + 2, 4), 3 - c
+    peers = (beside, across, corner)
 
     def load_slot(src):
         return [pltpu.make_async_copy(src.at[pl.ds(i * 512, 512)], slot.at[pl.ds(i * 512, 512)], slot_sem.at[i]) for i in range(2)]
@@ -60,21 +66,54 @@
         k = (ti if g == 0 else 1 - ti) * 4 + ci
         return k, 15 - k
 
-    def send_kv(l, hop, g, i, ci):
-        rows = pl.ds(pl.multiple_of(segments(g, t, ci)[i] * SEG, SEG), SEG)
+    def send_half(i, j):
+        place = (j, pl.ds(i * SEG, SEG))
+        return pltpu.make_async_remote_copy(sbuf.at[place], rbuf.at[place], ds_sem.at[i, j], dr_sem.at[i, j], other, MESH)
+
+    def send_o(g):
+        return pltpu.make_async_remote_copy(o_ref.at[g], o_x.at[1 - g], os_sem.at[g], or_sem.at[1 - g], other, MESH)
+
+    def recv_o(g):
+        return pltpu.make_async_remote_copy(o_ref.at[g], o_x.at[g], os_sem.at[g], or_sem.at[g], other, MESH)
+
+    def send_kv(l, kind, g, i, owner, to):
+        rows = pl.ds(pl.multiple_of(segments(g, t, owner)[i] * SEG, SEG), SEG)
         place = kv.at[l, rows, :]
-        return pltpu.make_async_remote_copy(place, place, ks_sem.at[l, hop, g, i], kr_sem.at[l, hop, g, i],
-                                            {'cp': lax.rem(c + hop + 1, 4)}, MESH)
+        return pltpu.make_async_remote_copy(place, place, ks_sem.at[l, kind, g, i], kr_sem.at[l, kind, g, i], {'cp': to}, MESH)
+
+    def piece(owner, p):
+        return pl.ds(pl.multiple_of(owner * (PIECES * PIECE) + p * PIECE, PIECE), PIECE)
+
+    def send_wo(p):
+        return pltpu.make_async_remote_copy(wo.at[1, piece(c, p)], wo_x.at[piece(c, p)], ws_sem.at[p], wr_sem.at[p], other, MESH)
+
+    def spread_wo(kind, p, owner, to):
+        place = wo_x.at[piece(owner, p)]
+        return pltpu.make_async_remote_copy(place, place, fs_sem.at[kind, p], fr_sem.at[kind, p], {'cp': to}, MESH)
+
+    def pass_wo(pieces):
+        for p in pieces:
+            send_wo(p).wait_recv()
+            spread_wo(1, p, c, across).start()
+            spread_wo(0, p, c, beside).start()
+
+    def relay_wo(pieces):
+        for p in pieces:
+            spread_wo(1, p, across, across).wait_recv()
+            spread_wo(2, p, across, beside).start()
 
     tok = [pltpu.make_async_copy(tokens.at[:, pl.ds(j * CH, CH)], x_own.at[j], tok_sem.at[j]) for j in range(NCH)]
     start(tok)
+    turn = [pltpu.make_async_copy(table.at[pl.ds(pl.multiple_of(segments(g, t, c)[i] * SEG, SEG), SEG)],
+                                  turns.at[g, pl.ds(i * SEG, SEG)], turn_sem.at[g, i]) for g in range(2) for i in range(2)]
+    start(turn)
     start(load_kvw(0))
     start(load_slot(wq.at[0]))
 
     barrier = pltpu.get_barrier_semaphore()
     pl.semaphore_signal(barrier, inc=1, device_id=other, device_id_type=MESH)
-    for hop in range(3):
-        pl.semaphore_signal(barrier, inc=1, device_id={'cp': lax.rem(c + hop + 1, 4)}, device_id_type=MESH)
+    for to in peers:
+        pl.semaphore_signal(barrier, inc=1, device_id={'cp': to}, device_id_type=MESH)
     pl.semaphore_wait(barrier, 4)
     for j in range(NCH):
         send_x(tokens.at[:, pl.ds(j * CH, CH)], j).start()
@@ -90,7 +129,13 @@
     diff = (lax.broadcasted_iota(jnp.int32, (4 * SEG, 512), 1)
             - lax.broadcasted_iota(jnp.int32, (4 * SEG, 512), 0) % SEG)
 
-    def norm(x_ref, gain, g):
+    wait(turn)
+    for g in range(2):
+        near, far = turns[g], pltpu.roll(turns[g], HEAD, 1)
+        cos_ref[g] = jnp.where(low, near, far)
+        sin_ref[g] = jnp.where(low, far, near)
+
+    def norm(x_ref, gain_ref, l):
         total = jnp.zeros((ROWS, 1), F32)
         for j in range(NCH):
             x = x_ref[j].astype(F32)
@@ -98,25 +143,25 @@
         inv = lax.rsqrt(total * (1.0 / D) + 1e-5)
         for j in range(NCH):
             cols = pl.ds(j * CH, CH)
-            a_ref[g, :, cols] = (x_ref[j].astype(F32) * inv * gain[:, cols]).astype(BF16)
+            a_ref[:, cols] = (x_ref[j].astype(F32) * inv * gain_ref[l:l + 1, cols].astype(F32)).astype(BF16)
 
     def rope(v, g):
         swapped = jnp.where(first_half, pltpu.roll(v, 128 - HEAD // 2, 1), pltpu.roll(v, HEAD // 2, 1))
         return v * cos_ref[g] + swapped * sin_ref[g]
 
     def qkv(l, g):
-        k_new = jnp.dot(a_ref[g], wk_v[...], preferred_element_type=F32)
-        v_new = jnp.dot(a_ref[g], wv_v[...], preferred_element_type=F32).astype(BF16)
+        k_new = jnp.dot(a_ref[...], wk_v[...], preferred_element_type=F32)
+        v_new = jnp.dot(a_ref[...], wv_v[...], preferred_element_type=F32).astype(BF16)
         k_new = jnp.concatenate([rope(k_new[:, :128], g), rope(k_new[:, 128:], g)], axis=1).astype(BF16)
         for i in range(2):
             rows = pl.ds(pl.multiple_of(segments(g, t, c)[i] * SEG, SEG), SEG)
             kv[l, rows, 0:256] = k_new[i * SEG:(i + 1) * SEG]
             kv[l, rows, 256:512] = v_new[i * SEG:(i + 1) * SEG]
         for i in range(2):
-            for hop in (1, 0, 2):
-                send_kv(l, hop, g, i, c).start()
+            for kind in ((1, 2, 0) if g == 0 else (1, 0)):
+                send_kv(l, kind, g, i, c, peers[kind]).start()
         for h in range(4):
-            q = lax.dot_general(a_ref[g], slot[h * 256:(h + 1) * 256, :], (((1,), (1,)), ((), ())), preferred_element_type=F32)
+            q = lax.dot_general(a_ref[...], slot[h * 256:(h + 1) * 256, :], (((1,), (1,)), ((), ())), preferred_element_type=F32)
             for pair in range(2):
                 both = rope(q[:, pair * 128:(pair + 1) * 128], g)
                 turned = pltpu.roll(both, HEAD, 1)
@@ -127,8 +172,8 @@
                     for i in range(2):
                         qh[g, i, h, n * SEG:(n + 1) * SEG, :] = value[i * SEG:(i + 1) * SEG]
 
-    def attention(l, g):
-        for i in range(2):
+    def attention(l, g, parts=(0, 1)):
+        for i in parts:
             seg = segments(g, t, c)[i]
             free = 512 * i
             visible = diff <= seg * SEG - free
@@ -168,82 +213,139 @@
         return jnp.dot(lhs, slot[:, pl.ds(pl.multiple_of(j * CH, CH), CH)], preferred_element_type=F32)
 
     def reduce_chunk(own, j):
-        send_part(j).wait_recv()
         return (x_own[j].astype(F32) + (own + rbuf[j])).astype(BF16)
 
     for l in range(LAYERS):
         last = l == LAYERS - 1
         if l == 0:
             wait(tok)
-        norm(x_own, gain_attn[l], 0)
+        norm(x_own, gain_attn, l)
         wait(load_kvw(l))
         wait(load_slot(wq.at[l]))
         qkv(l, 0)
         for j in range(NCH):
             send_x(x_own.at[j], j).wait_recv()
-        norm(x_par, gain_attn[l], 1)
+        norm(x_par, gain_attn, l)
         qkv(l, 1)
         start(load_slot(wo.at[l]))
         if not last:
             start(load_kvw(l + 1))
+        for p in FIRST if not last else LATE:
+            send_wo(p).start()
+        for i in range(2):
+            send_kv(l, 1, 1, i, across, across).wait_recv()
+            send_kv(l, 2, 1, i, across, beside).start()
         for g in range(2):
             for i in range(2):
-                for hop in range(3):
-                    send_kv(l, hop, g, i, lax.rem(c + 3 - hop, 4)).wait_recv()
-        attention(l, 1)
-        wait(load_slot(wo.at[l]))
-
-        def o_send(j, carry, l=l):
-            part = slot_chunk(o_ref[1], j)
-            if l > 0:
+                for kind in range(3):
+                    if (kind, g) != (1, 1):
+                        send_kv(l, kind, g, i, peers[kind], peers[kind]).wait_recv()
+
+        if not last:
+            wait(load_slot(wo.at[l]))
+            for i in range(2):
+                attention(l, 1, (i,))
+
+                def o_send(j, carry, i=i):
+                    rows = pl.ds(i * SEG, SEG)
+                    sbuf[j, rows] = slot_chunk(o_ref[1, rows], j)
+                    send_half(i, j).start()
+                    return carry
+                lax.fori_loop(0, NCH, o_send, 0)
+            pass_wo(FIRST)
+            attention(l, 0)
+
+            def o_reduce(j, carry):
+                own = slot_chunk(o_ref[0], j)
+                send_half(0, j).wait_recv()
+                send_half(1, j).wait_recv()
+                new = reduce_chunk(own, j)
+                send_x(x_own.at[j], j).wait_send()
+                x_own[j] = new
+                send_x(x_own.at[j], j).start()
+                return carry
+            lax.fori_loop(0, NCH, o_reduce, 0)
+            relay_wo(FIRST)
+            start(load_slot(wq.at[l + 1]))
+        else:
+            pass_wo(LATE)
+            attention(l, 0)
+            send_o(0).start()
+            attention(l, 1)
+            send_o(1).start()
+            relay_wo(LATE)
+            wait(load_slot(wo.at[l]))
+
+            def o_near(j, carry):
                 send_part(j).wait_send()
-            sbuf[j] = part
-            send_part(j).start()
-            return carry
-        lax.fori_loop(0, NCH, o_send, 0)
-        attention(l, 0)
-
-        def o_reduce(j, carry):
-            new = reduce_chunk(slot_chunk(o_ref[0], j), j)
-            send_x(x_own.at[j], j).wait_send()
-            x_own[j] = new
-            send_x(x_own.at[j], j).start()
-            return carry
-        lax.fori_loop(0, NCH, o_reduce, 0)
-        if not last:
-            start(load_slot(wq.at[l + 1]))
+                sbuf[j] = slot_chunk(o_ref[1], j)
+                return carry
+            lax.fori_loop(0, NCH, o_near, 0)
+            for p in range(PIECES):
+                spread_wo(0, p, beside, beside).wait_recv()
+                spread_wo(2, p, corner, beside).wait_recv()
 
         def gate_up(g, l=l, last=last):
             def step(j, carry):
-                if g == 0:
+                if g == (1 if last else 0):
                     wait(load_gu(l, j))
-                gate = jnp.dot(a_ref[g], wg_v[j], preferred_element_type=F32)
-                up = jnp.dot(a_ref[g], wu_v[j], preferred_element_type=F32)
+                gate = jnp.dot(a_ref[...], wg_v[j], preferred_element_type=F32)
+                up = jnp.dot(a_ref[...], wu_v[j], preferred_element_type=F32)
                 act[g, :, pl.ds(pl.multiple_of(j * GCH, GCH), GCH)] = (gate * jax.nn.sigmoid(gate) * up).astype(BF16)
                 if g == 1 and not last:
                     start(load_gu(l + 1, j))
                 return carry
             lax.fori_loop(0, NGC, step, 0)
 
-        norm(x_own, gain_mlp[l], 0)
-        gate_up(0)
-        for j in range(NCH):
-            send_x(x_own.at[j], j).wait_recv()
-        norm(x_par, gain_mlp[l], 1)
-        gate_up(1)
+        def far_chunk(g, j):
+            return jnp.dot(o_x[g], wo_x[:, pl.ds(pl.multiple_of(j * CH, CH), CH)], preferred_element_type=F32)
+
+        if not last:
+            norm(x_own, gain_mlp, l)
+            gate_up(0)
+            for j in range(NCH):
+                send_x(x_own.at[j], j).wait_recv()
+            for p in MIDDLE:
+                send_wo(p).start()
+            norm(x_par, gain_mlp, l)
+            gate_up(1)
+        else:
+            recv_o(1).wait_recv()
+
+            def o_far(j, carry):
+                x_par[j] = (x_par[j].astype(F32) + (sbuf[j] + far_chunk(1, j))).astype(BF16)
+                return carry
+            lax.fori_loop(0, NCH, o_far, 0)
+            norm(x_par, gain_mlp, l)
+            gate_up(1)
 
         def down_chunk(g, j, l=l):
             load_wd(l, j).wait()
             return jnp.dot(act[g], wd_v[lax.rem(j, RING)], preferred_element_type=F32)
 
-        def down_send(j, carry, l=l):
+        def down_send(j, carry, l=l, last=last):
             part = down_chunk(1, j)
             load_wd(l, lax.rem(j + RING, NCH)).start()
-            send_part(j).wait_send()
+            if not last:
+                send_half(0, j).wait_send()
+                send_half(1, j).wait_send()
             sbuf[j] = part
             send_part(j).start()
             return carry
         lax.fori_loop(0, NCH, down_send, 0)
+        if not last:
+            pass_wo(MIDDLE)
+        else:
+            recv_o(0).wait_recv()
+
+            def o_own(j, carry):
+                new = (x_own[j].astype(F32) + (slot_chunk(o_ref[0], j) + far_chunk(0, j))).astype(BF16)
+                send_x(x_own.at[j], j).wait_send()
+                x_own[j] = new
+                return carry
+            lax.fori_loop(0, NCH, o_own, 0)
+            norm(x_own, gain_mlp, l)
+            gate_up(0)
 
         def down_reduce(j, carry, l=l, last=last):
             own = down_chunk(0, j)
@@ -259,8 +361,10 @@
                 @pl.when(j >= NCH - RING)
                 def _():
                     load_wd(l + 1, j + RING - NCH).start()
+            send_part(j).wait_recv()
             new = reduce_chunk(own, j)
-            send_x(x_own.at[j], j).wait_send()
+            if not last:
+                send_x(x_own.at[j], j).wait_send()
             x_own[j] = new
             cols = pl.ds(pl.multiple_of(j * CH, CH), CH)
             if last:
@@ -269,6 +373,8 @@
                 send_x(x_own.at[j], j).start()
             return carry
         lax.fori_loop(0, NCH, down_reduce, 0)
+        if not last:
+            relay_wo(MIDDLE)
 
     for j in range(NCH):
         send_part(j).wait_send()
@@ -276,8 +382,21 @@
     for l in range(LAYERS):
         for g in range(2):
             for i in range(2):
-                for hop in range(3):
-                    send_kv(l, hop, g, i, c).wait_send()
+                for kind in range(3):
+                    send_kv(l, kind, g, i, c, beside).wait_send()
+    for g in range(2):
+        send_o(g).wait_send()
+    for p in range(PIECES):
+        send_wo(p).wait_send()
+        for kind in range(3):
+            spread_wo(kind, p, c, beside).wait_send()
+
+
+def turn_table():
+    inv_freq = np.float32(500000.0) ** (-(np.arange(HEAD // 2, dtype=np.float32) * np.float32(2.0) / np.float32(HEAD)))
+    angles = np.arange(16 * SEG, dtype=np.float32)[:, None] * inv_freq.astype(np.float32)[None, :]
+    cos, sin = np.cos(angles), np.sin(angles)
+    return np.concatenate([cos, cos, -sin, sin], axis=1).astype(np.float32)
 
 
 def solution(mesh):
@@ -291,16 +410,6 @@
     down_spec = P(None, 'tp', None)
 
     def body(tokens, norm_attn, norm_mlp, w_q, w_k, w_v, w_o, w_gate, w_up, w_down):
-        t = lax.axis_index('tp')
-        c = lax.axis_index('cp')
-        dev = jnp.stack([t, 1 - t]) * cp_size + c
-        seg = jnp.stack([dev, 2 * tp_size * cp_size - 1 - dev], axis=1)
-        pos = (seg[:, :, None] * SEG + jnp.arange(SEG)[None, None, :]).reshape(2, ROWS)
-        inv_freq = 500000.0 ** (-(jnp.arange(HEAD // 2, dtype=F32) * 2.0 / HEAD))
-        angles = pos.astype(F32)[:, :, None] * inv_freq
-        cos, sin = jnp.cos(angles), jnp.sin(angles)
-        cos = jnp.concatenate([cos, cos, cos, cos], axis=-1)
-        sin = jnp.concatenate([-sin, sin, -sin, sin], axis=-1)
         wq = jnp.transpose(w_q, (0, 2, 3, 1)).reshape(LAYERS, 1024, D)
         wo = w_o.reshape(LAYERS, 1024, D)
         hbm = pl.BlockSpec(memory_space=pl.ANY)
@@ -309,32 +418,38 @@
         return pl.pallas_call(
             kernel,
             out_shape=jax.ShapeDtypeStruct((ROWS, D), BF16),
-            in_specs=[hbm, vmem, vmem, vmem, vmem] + [hbm] * 7,
+            in_specs=[hbm, vmem, vmem] + [hbm] * 8,
             out_specs=hbm,
             scratch_shapes=[
                 pltpu.VMEM((NCH, ROWS, CH), BF16),
                 pltpu.VMEM((NCH, ROWS, CH), BF16),
-                pltpu.VMEM((2, ROWS, D), BF16),
+                pltpu.VMEM((ROWS, D), BF16),
                 pltpu.VMEM((2, 2, 4, 4 * SEG, 128), BF16),
+                pltpu.VMEM((2, ROWS, 1024), BF16),
                 pltpu.VMEM((2, ROWS, 1024), BF16),
                 pltpu.VMEM((LAYERS, 1024, 512), BF16),
                 pltpu.VMEM((2, ROWS, FF), BF16),
                 pltpu.VMEM((NCH, ROWS, CH), F32),
                 pltpu.VMEM((NCH, ROWS, CH), F32),
                 pltpu.VMEM((1024, D), BF16),
+                pltpu.VMEM((1024, D), BF16),
                 pltpu.VMEM((D, 256), BF16),
                 pltpu.VMEM((D, 256), BF16),
                 pltpu.VMEM((NGC, D, GCH), BF16),
                 pltpu.VMEM((NGC, D, GCH), BF16),
                 pltpu.VMEM((RING, FF, CH), BF16),
-                dma((NCH,)), dma((NCH,)), dma((2,)), dma((2,)), dma((2, NGC)), dma((RING,)),
-                dma((NCH,)), dma((NCH,)), dma((NCH,)), dma((NCH,)),
-                dma((LAYERS, 3, 2, 2)), dma((LAYERS, 3, 2, 2)),
+                pltpu.VMEM((2, ROWS, 128), F32),
+                pltpu.VMEM((2, ROWS, 128), F32),
+                pltpu.VMEM((2, ROWS, 128), F32),
+                dma((NCH,)), dma((NCH,)), dma((2,)), dma((2,)), dma((2, NGC)), dma((RING,)), dma((2, 2)),
+                dma((NCH,)), dma((NCH,)), dma((NCH,)), dma((NCH,)), dma((2, NCH)), dma((2, NCH)),
+                dma((LAYERS, 3, 2, 2)), dma((LAYERS, 3, 2, 2)), dma((2,)), dma((2,)),
+                dma((PIECES,)), dma((PIECES,)), dma((3, PIECES)), dma((3, PIECES)),
             ],
             compiler_params=pltpu.CompilerParams(
                 collective_id=0, has_side_effects=True, vmem_limit_bytes=67_000_000),
             name='decoder',
-        )(tokens, norm_attn.astype(F32).reshape(LAYERS, 1, D), norm_mlp.astype(F32).reshape(LAYERS, 1, D), cos, sin,
+        )(tokens, norm_attn, norm_mlp, jnp.asarray(turn_table()),
           wq, w_k, w_v, wo, w_gate, w_up, w_down)
 
     return jax.shard_map(

time: 196 us -> 166 us (0.85)
  Pallas kernels: 190 us -> 164 us
  local copies, waits for them, and re-layouts: 4.74 us -> 1.88 us
    pallas_call x1, Pallas kernels: 190 us -> 164 us  [body(): pl.pallas_call(kernel, out_shape=jax.ShapeDtypeStruct((ROWS, D), BF16), i...]
    reshape x2 -> x0, local copies, waits for them, and re-layouts: 2.62 us -> none  [the longest x1 1.31 us: body(): norm_attn.astype(F32).reshape(LAYERS, 1, D)]
where the time goes in v3:
time: 166 us; the launch traced here: 165 us
  Pallas kernels  164 us (99%)
  local copies, waits for them, and re-layouts  1.88 us (1%)
    pallas_call x1, Pallas kernels, body(): pl.pallas_call(kernel, out_shape=jax.ShapeDtypeStruct((ROWS, D), BF16), i...  164 us

profile of v3, /device:TPU:0, one launch (start us, length us, event | category | flops | bytes accessed | tf_op | source)
XLA Modules:
  0.0 165.5 jit_solution(10860612741035984899)
XLA Ops:
  0.0 163.6 %decoder.1 = bf16[128,2048]{1,0:T(8,128)(2,1)} custom-call(bf16[128,2048]{1,0:T(8,128)(2,1)} %tokens.1, bf16[2,2048]{1,0:T(2,128)(2,1)} %gain_attn.1, bf16[2,2048]{1,0:T(2,128)(2,1)} %gain_mlp.1, f32[1024,128]{1,0:T(8,128)} %constant.2.clone.table, bf16[2,1024,2048]{2,1,0:T(8,128)(2,1)} %bitcast.4, bf16[2,2048,256]{2,1,0:T(8,128)(2,1)} %wk.1, ...), custom_call_target="tpu_custom_call" | custom-call | tf_op jit(solution)/shard_map/decoder/pallas_call | solution.py:418
  163.6 1.9 %copy.13 = bf16[128,2048]{1,0:T(8,128)(2,1)} copy(bf16[128,2048]{1,0:T(8,128)(2,1)} %decoder.1) | data formatting | bytes 1048576

commit v4 on v3

--- a/solution.py
+++ b/solution.py
@@ -15,8 +15,8 @@
 CH, NCH = 256, 8
 GCH, NGC = 512, 8
 RING = 4
-PIECES, PIECE = 8, 32
-FIRST, MIDDLE, LATE = (0, 1, 2, 3), (4, 5), (6, 7)
+PIECES, PIECE = 16, 16
+FIRST, MIDDLE, LATE = range(0, 6), range(6, 10), range(10, 16)
 LAYERS = 2
 EXP2_SCALE = math.log2(math.e) / math.sqrt(HEAD)
 
@@ -117,6 +117,8 @@
     pl.semaphore_wait(barrier, 4)
     for j in range(NCH):
         send_x(tokens.at[:, pl.ds(j * CH, CH)], j).start()
+    for p in FIRST:
+        send_wo(p).start()
     for j in range(NGC):
         start(load_gu(0, j))
     for j in range(RING):
@@ -230,20 +232,20 @@
         start(load_slot(wo.at[l]))
         if not last:
             start(load_kvw(l + 1))
-        for p in FIRST if not last else LATE:
-            send_wo(p).start()
         for i in range(2):
             send_kv(l, 1, 1, i, across, across).wait_recv()
             send_kv(l, 2, 1, i, across, beside).start()
-        for g in range(2):
-            for i in range(2):
-                for kind in range(3):
-                    if (kind, g) != (1, 1):
-                        send_kv(l, kind, g, i, peers[kind], peers[kind]).wait_recv()
-
+
+        def wait_kv(i, l=l):
+            for kind, g in ((0, 0), (1, 0), (2, 0), (0, 1), (2, 1)):
+                send_kv(l, kind, g, i, peers[kind], peers[kind]).wait_recv()
+
+        wait_kv(0)
         if not last:
             wait(load_slot(wo.at[l]))
             for i in range(2):
+                if i == 1:
+                    wait_kv(1)
                 attention(l, 1, (i,))
 
                 def o_send(j, carry, i=i):
@@ -265,15 +267,23 @@
                 send_x(x_own.at[j], j).start()
                 return carry
             lax.fori_loop(0, NCH, o_reduce, 0)
+            for p in MIDDLE:
+                send_wo(p).start()
             relay_wo(FIRST)
             start(load_slot(wq.at[l + 1]))
         else:
-            pass_wo(LATE)
-            attention(l, 0)
+            pass_wo(LATE[:2])
+            attention(l, 0, (0,))
+            wait_kv(1)
+            attention(l, 0, (1,))
             send_o(0).start()
-            attention(l, 1)
+            pass_wo(LATE[2:5])
+            relay_wo(LATE[:2])
+            attention(l, 1, (0,))
+            pass_wo(LATE[5:])
+            attention(l, 1, (1,))
             send_o(1).start()
-            relay_wo(LATE)
+            relay_wo(LATE[2:5])
             wait(load_slot(wo.at[l]))
 
             def o_near(j, carry):
@@ -281,6 +291,7 @@
                 sbuf[j] = slot_chunk(o_ref[1], j)
                 return carry
             lax.fori_loop(0, NCH, o_near, 0)
+            relay_wo(LATE[5:])
             for p in range(PIECES):
                 spread_wo(0, p, beside, beside).wait_recv()
                 spread_wo(2, p, corner, beside).wait_recv()
@@ -305,8 +316,6 @@
             gate_up(0)
             for j in range(NCH):
                 send_x(x_own.at[j], j).wait_recv()
-            for p in MIDDLE:
-                send_wo(p).start()
             norm(x_par, gain_mlp, l)
             gate_up(1)
         else:
@@ -374,6 +383,8 @@
             return carry
         lax.fori_loop(0, NCH, down_reduce, 0)
         if not last:
+            for p in LATE:
+                send_wo(p).start()
             relay_wo(MIDDLE)
 
     for j in range(NCH):

time: 166 us -> 163 us (0.982)
  Pallas kernels: 164 us -> 161 us
    pallas_call x1, Pallas kernels: 164 us -> 161 us  [body(): pl.pallas_call(kernel, out_shape=jax.ShapeDtypeStruct((ROWS, D), BF16), i...]
where the time goes in v4:
time: 163 us
  Pallas kernels  161 us (99%)
  local copies, waits for them, and re-layouts  1.88 us (1%)
    pallas_call x1, Pallas kernels, body(): pl.pallas_call(kernel, out_shape=jax.ShapeDtypeStruct((ROWS, D), BF16), i...  161 us

profile of v4, /device:TPU:0, one launch (start us, length us, event | category | flops | bytes accessed | tf_op | source)
XLA Modules:
  0.0 163.0 jit_solution(1277861126209743068)
XLA Ops:
  0.0 161.1 %decoder.1 = bf16[128,2048]{1,0:T(8,128)(2,1)} custom-call(bf16[128,2048]{1,0:T(8,128)(2,1)} %tokens.1, bf16[2,2048]{1,0:T(2,128)(2,1)} %gain_attn.1, bf16[2,2048]{1,0:T(2,128)(2,1)} %gain_mlp.1, f32[1024,128]{1,0:T(8,128)} %constant.2.clone.table, bf16[2,1024,2048]{2,1,0:T(8,128)(2,1)} %bitcast.4, bf16[2,2048,256]{2,1,0:T(8,128)(2,1)} %wk.1, ...), custom_call_target="tpu_custom_call" | custom-call | tf_op jit(solution)/shard_map/decoder/pallas_call | solution.py:429
  161.1 1.9 %copy.13 = bf16[128,2048]{1,0:T(8,128)(2,1)} copy(bf16[128,2048]{1,0:T(8,128)(2,1)} %decoder.1) | data formatting | bytes 1048576

commit v5 on v4

--- a/solution.py
+++ b/solution.py
@@ -1,3 +1,4 @@
+import functools
 import math
 
 import jax
@@ -16,7 +17,7 @@
 GCH, NGC = 512, 8
 RING = 4
 PIECES, PIECE = 16, 16
-FIRST, MIDDLE, LATE = range(0, 6), range(6, 10), range(10, 16)
+FIRST, MIDDLE, LATE = range(0, 7), range(7, 12), range(12, 16)
 LAYERS = 2
 EXP2_SCALE = math.log2(math.e) / math.sqrt(HEAD)
 
@@ -70,11 +71,13 @@
         place = (j, pl.ds(i * SEG, SEG))
         return pltpu.make_async_remote_copy(sbuf.at[place], rbuf.at[place], ds_sem.at[i, j], dr_sem.at[i, j], other, MESH)
 
-    def send_o(g):
-        return pltpu.make_async_remote_copy(o_ref.at[g], o_x.at[1 - g], os_sem.at[g], or_sem.at[1 - g], other, MESH)
-
-    def recv_o(g):
-        return pltpu.make_async_remote_copy(o_ref.at[g], o_x.at[g], os_sem.at[g], or_sem.at[g], other, MESH)
+    def send_o(g, i):
+        rows = pl.ds(i * SEG, SEG)
+        return pltpu.make_async_remote_copy(o_ref.at[g, rows], o_x.at[1 - g, rows], os_sem.at[g, i], or_sem.at[1 - g, i], other, MESH)
+
+    def recv_o(g, i):
+        rows = pl.ds(i * SEG, SEG)
+        return pltpu.make_async_remote_copy(o_ref.at[g, rows], o_x.at[g, rows], os_sem.at[g, i], or_sem.at[g, i], other, MESH)
 
     def send_kv(l, kind, g, i, owner, to):
         rows = pl.ds(pl.multiple_of(segments(g, t, owner)[i] * SEG, SEG), SEG)
@@ -119,8 +122,6 @@
         send_x(tokens.at[:, pl.ds(j * CH, CH)], j).start()
     for p in FIRST:
         send_wo(p).start()
-    for j in range(NGC):
-        start(load_gu(0, j))
     for j in range(RING):
         load_wd(0, j).start()
 
@@ -179,26 +180,25 @@
             seg = segments(g, t, c)[i]
             free = 512 * i
             visible = diff <= seg * SEG - free
-            for parity in range(2):
-                def pair_step(p, carry, i=i, free=free, visible=visible, parity=parity):
-                    h = 2 * p + parity
-                    k_cols = pl.ds(pl.multiple_of(p * 128, 128), 128)
-                    v_cols = pl.ds(pl.multiple_of(256 + p * 128, 128), 128)
-                    q = qh[g, i, h]
-                    nt = (((1,), (1,)), ((), ()))
-                    s_end = lax.dot_general(q, kv[l, pl.ds(free, 512), k_cols], nt, preferred_element_type=F32)
-                    s_end = jnp.where(visible, s_end, -jnp.inf)
-                    top = jnp.max(s_end, axis=-1, keepdims=True)
-                    if free:
-                        s_free = lax.dot_general(q, kv[l, pl.ds(0, free), k_cols], nt, preferred_element_type=F32)
-                        top = jnp.maximum(top, jnp.max(s_free, axis=-1, keepdims=True))
-                    e_end = jnp.exp2((s_end - top) * EXP2_SCALE)
-                    total = jnp.sum(e_end, axis=-1, keepdims=True)
-                    mixed = jnp.dot(e_end.astype(BF16), kv[l, pl.ds(free, 512), v_cols], preferred_element_type=F32)
-                    if free:
-                        e_free = jnp.exp2((s_free - top) * EXP2_SCALE)
-                        total = total + jnp.sum(e_free, axis=-1, keepdims=True)
-                        mixed = mixed + jnp.dot(e_free.astype(BF16), kv[l, pl.ds(0, free), v_cols], preferred_element_type=F32)
+
+            def pair_step(p, carry, i=i, free=free, visible=visible):
+                k_cols = pl.ds(pl.multiple_of(p * 128, 128), 128)
+                v_cols = pl.ds(pl.multiple_of(256 + p * 128, 128), 128)
+                nt = (((1,), (1,)), ((), ()))
+                spans = ((free, 512), (0, 512)) if free else ((free, 512),)
+                scores, tops, totals, outs = {}, {}, {}, {}
+                for parity in range(2):
+                    q = qh[g, i, 2 * p + parity]
+                    for n, (lo, size) in enumerate(spans):
+                        s = lax.dot_general(q, kv[l, pl.ds(lo, size), k_cols], nt, preferred_element_type=F32)
+                        scores[parity, n] = jnp.where(visible, s, -jnp.inf) if n == 0 else s
+                for parity in range(2):
+                    tops[parity] = functools.reduce(jnp.maximum, [jnp.max(scores[parity, n], axis=-1, keepdims=True) for n in range(len(spans))])
+                    total, mixed = 0.0, 0.0
+                    for n, (lo, size) in enumerate(spans):
+                        e = jnp.exp2((scores[parity, n] - tops[parity]) * EXP2_SCALE)
+                        total = total + jnp.sum(e, axis=-1, keepdims=True)
+                        mixed = mixed + jnp.dot(e.astype(BF16), kv[l, pl.ds(lo, size), v_cols], preferred_element_type=F32)
                     mixed = mixed / total
                     for pair in range(2):
                         sides = []
@@ -206,10 +206,10 @@
                             n = pair * 2 + odd
                             value = mixed[n * SEG:(n + 1) * SEG]
                             sides.append(value if odd == parity else pltpu.roll(value, HEAD, 1))
-                        cols = pl.ds(pl.multiple_of(h * 256 + pair * 128, 128), 128)
+                        cols = pl.ds(pl.multiple_of((2 * p + parity) * 256 + pair * 128, 128), 128)
                         o_ref[g, i * SEG:(i + 1) * SEG, cols] = jnp.where(low_seg, sides[0], sides[1]).astype(BF16)
-                    return carry
-                lax.fori_loop(0, 2, pair_step, 0)
+                return carry
+            lax.fori_loop(0, 2, pair_step, 0)
 
     def slot_chunk(lhs, j):
         return jnp.dot(lhs, slot[:, pl.ds(pl.multiple_of(j * CH, CH), CH)], preferred_element_type=F32)
@@ -232,9 +232,13 @@
         start(load_slot(wo.at[l]))
         if not last:
             start(load_kvw(l + 1))
+        if last:
+            pass_wo(LATE[:1])
         for i in range(2):
             send_kv(l, 1, 1, i, across, across).wait_recv()
             send_kv(l, 2, 1, i, across, beside).start()
+            if last and i == 0:
+                pass_wo(LATE[1:3])
 
         def wait_kv(i, l=l):
             for kind, g in ((0, 0), (1, 0), (2, 0), (0, 1), (2, 1)):
@@ -259,6 +263,7 @@
 
             def o_reduce(j, carry):
                 own = slot_chunk(o_ref[0], j)
+                start(load_gu(0, j))
                 send_half(0, j).wait_recv()
                 send_half(1, j).wait_recv()
                 new = reduce_chunk(own, j)
@@ -272,18 +277,18 @@
             relay_wo(FIRST)
             start(load_slot(wq.at[l + 1]))
         else:
-            pass_wo(LATE[:2])
+            pass_wo(LATE[3:])
             attention(l, 0, (0,))
+            send_o(0, 0).start()
             wait_kv(1)
             attention(l, 0, (1,))
-            send_o(0).start()
-            pass_wo(LATE[2:5])
-            relay_wo(LATE[:2])
+            send_o(0, 1).start()
+            relay_wo(LATE[:1])
             attention(l, 1, (0,))
-            pass_wo(LATE[5:])
+            send_o(1, 0).start()
+            relay_wo(LATE[1:])
             attention(l, 1, (1,))
-            send_o(1).start()
-            relay_wo(LATE[2:5])
+            send_o(1, 1).start()
             wait(load_slot(wo.at[l]))
 
             def o_near(j, carry):
@@ -291,7 +296,6 @@
                 sbuf[j] = slot_chunk(o_ref[1], j)
                 return carry
             lax.fori_loop(0, NCH, o_near, 0)
-            relay_wo(LATE[5:])
             for p in range(PIECES):
                 spread_wo(0, p, beside, beside).wait_recv()
                 spread_wo(2, p, corner, beside).wait_recv()
@@ -303,8 +307,6 @@
                 gate = jnp.dot(a_ref[...], wg_v[j], preferred_element_type=F32)
                 up = jnp.dot(a_ref[...], wu_v[j], preferred_element_type=F32)
                 act[g, :, pl.ds(pl.multiple_of(j * GCH, GCH), GCH)] = (gate * jax.nn.sigmoid(gate) * up).astype(BF16)
-                if g == 1 and not last:
-                    start(load_gu(l + 1, j))
                 return carry
             lax.fori_loop(0, NGC, step, 0)
 
@@ -319,7 +321,8 @@
             norm(x_par, gain_mlp, l)
             gate_up(1)
         else:
-            recv_o(1).wait_recv()
+            recv_o(1, 0).wait_recv()
+            recv_o(1, 1).wait_recv()
 
             def o_far(j, carry):
                 x_par[j] = (x_par[j].astype(F32) + (sbuf[j] + far_chunk(1, j))).astype(BF16)
@@ -345,7 +348,8 @@
         if not last:
             pass_wo(MIDDLE)
         else:
-            recv_o(0).wait_recv()
+            recv_o(0, 0).wait_recv()
+            recv_o(0, 1).wait_recv()
 
             def o_own(j, carry):
                 new = (x_own[j].astype(F32) + (slot_chunk(o_ref[0], j) + far_chunk(0, j))).astype(BF16)
@@ -370,6 +374,8 @@
                 @pl.when(j >= NCH - RING)
                 def _():
                     load_wd(l + 1, j + RING - NCH).start()
+            if not last:
+                start(load_gu(l + 1, j))
             send_part(j).wait_recv()
             new = reduce_chunk(own, j)
             if not last:
@@ -396,7 +402,8 @@
                 for kind in range(3):
                     send_kv(l, kind, g, i, c, beside).wait_send()
     for g in range(2):
-        send_o(g).wait_send()
+        send_o(g, 0).wait_send()
+        send_o(g, 1).wait_send()
     for p in range(PIECES):
         send_wo(p).wait_send()
         for kind in range(3):
@@ -454,7 +461,7 @@
                 pltpu.VMEM((2, ROWS, 128), F32),
                 dma((NCH,)), dma((NCH,)), dma((2,)), dma((2,)), dma((2, NGC)), dma((RING,)), dma((2, 2)),
                 dma((NCH,)), dma((NCH,)), dma((NCH,)), dma((NCH,)), dma((2, NCH)), dma((2, NCH)),
-                dma((LAYERS, 3, 2, 2)), dma((LAYERS, 3, 2, 2)), dma((2,)), dma((2,)),
+                dma((LAYERS, 3, 2, 2)), dma((LAYERS, 3, 2, 2)), dma((2, 2)), dma((2, 2)),
                 dma((PIECES,)), dma((PIECES,)), dma((3, PIECES)), dma((3, PIECES)),
             ],
             compiler_params=pltpu.CompilerParams(

time: 163 us -> 158 us (0.969)
  Pallas kernels: 161 us -> 156 us
    pallas_call x1, Pallas kernels: 161 us -> 156 us  [body(): pl.pallas_call(kernel, out_shape=jax.ShapeDtypeStruct((ROWS, D), BF16), i...]
where the time goes in v5:
time: 158 us; the launch traced here: 157 us
  Pallas kernels  156 us (99%)
  local copies, waits for them, and re-layouts  1.88 us (1%)
    pallas_call x1, Pallas kernels, body(): pl.pallas_call(kernel, out_shape=jax.ShapeDtypeStruct((ROWS, D), BF16), i...  156 us

profile of v5, /device:TPU:0, one launch (start us, length us, event | category | flops | bytes accessed | tf_op | source)
XLA Modules:
  0.0 157.5 jit_solution(6365557851503196924)
XLA Ops:
  0.0 155.6 %decoder.1 = bf16[128,2048]{1,0:T(8,128)(2,1)} custom-call(bf16[128,2048]{1,0:T(8,128)(2,1)} %tokens.1, bf16[2,2048]{1,0:T(2,128)(2,1)} %gain_attn.1, bf16[2,2048]{1,0:T(2,128)(2,1)} %gain_mlp.1, f32[1024,128]{1,0:T(8,128)} %constant.2.clone.table, bf16[2,1024,2048]{2,1,0:T(8,128)(2,1)} %bitcast.4, bf16[2,2048,256]{2,1,0:T(8,128)(2,1)} %wk.1, ...), custom_call_target="tpu_custom_call" | custom-call | tf_op jit(solution)/shard_map/decoder/pallas_call | solution.py:436
  155.6 1.9 %copy.13 = bf16[128,2048]{1,0:T(8,128)(2,1)} copy(bf16[128,2048]{1,0:T(8,128)(2,1)} %decoder.1) | data formatting | bytes 1048576

commit v6 on v5

--- a/solution.py
+++ b/solution.py
@@ -17,7 +17,7 @@
 GCH, NGC = 512, 8
 RING = 4
 PIECES, PIECE = 16, 16
-FIRST, MIDDLE, LATE = range(0, 7), range(7, 12), range(12, 16)
+FIRST, MIDDLE, LATE = range(0, 4), range(4, 9), range(9, 16)
 LAYERS = 2
 EXP2_SCALE = math.log2(math.e) / math.sqrt(HEAD)
 
@@ -25,8 +25,8 @@
 def kernel(tokens, gain_attn, gain_mlp, table, wq, wk, wv, wo, wg, wu, wd, out,
            x_own, x_par, a_ref, qh, o_ref, o_x, kv, act, sbuf, rbuf, slot, wo_x, wk_v, wv_v, wg_v, wu_v, wd_v,
            turns, cos_ref, sin_ref,
-           tok_sem, out_sem, slot_sem, kvw_sem, gu_sem, wd_sem, turn_sem, xs_sem, xr_sem, ps_sem, pr_sem, ds_sem, dr_sem,
-           ks_sem, kr_sem, os_sem, or_sem, ws_sem, wr_sem, fs_sem, fr_sem):
+           tok_sem, out_sem, slot_sem, kvw_sem, gu_sem, wd_sem, wo_sem, turn_sem, xs_sem, xr_sem, ps_sem, pr_sem, ds_sem, dr_sem,
+           ts_sem, tr_sem, ks_sem, kr_sem, os_sem, or_sem, ws_sem, wr_sem, fs_sem, fr_sem):
     t = lax.axis_index('tp')
     c = lax.axis_index('cp')
     other = {'tp': 1 - t}
@@ -59,6 +59,17 @@
 
     def send_x(src, j):
         return pltpu.make_async_remote_copy(src, x_par.at[j], xs_sem.at[j], xr_sem.at[j], other, MESH)
+
+    def send_tokens(i, j):
+        rows, cols = pl.ds(i * SEG, SEG), pl.ds(j * CH, CH)
+        return pltpu.make_async_remote_copy(tokens.at[rows, cols], x_par.at[j, rows], ts_sem.at[i, j], tr_sem.at[i, j], other, MESH)
+
+    def load_wo(j):
+        cols = pl.ds(pl.multiple_of(j * CH, CH), CH)
+        return pltpu.make_async_copy(wo.at[0, :, cols], wd_v.at[lax.rem(j, RING), wo_rows(j)], wo_sem.at[j])
+
+    def wo_rows(j):
+        return pl.ds(pl.multiple_of(j // RING * 1024, 1024), 1024)
 
     def send_part(j):
         return pltpu.make_async_remote_copy(sbuf.at[j], rbuf.at[j], ps_sem.at[j], pr_sem.at[j], other, MESH)
@@ -118,12 +129,13 @@
     for to in peers:
         pl.semaphore_signal(barrier, inc=1, device_id={'cp': to}, device_id_type=MESH)
     pl.semaphore_wait(barrier, 4)
-    for j in range(NCH):
-        send_x(tokens.at[:, pl.ds(j * CH, CH)], j).start()
+    for i in range(2):
+        for j in range(NCH):
+            send_tokens(i, j).start()
     for p in FIRST:
         send_wo(p).start()
-    for j in range(RING):
-        load_wd(0, j).start()
+    for j in range(NCH):
+        load_wo(j).start()
 
     lane = lax.broadcasted_iota(jnp.int32, (ROWS, 128), 1)
     first_half = (lane % HEAD) < HEAD // 2
@@ -138,42 +150,49 @@
         cos_ref[g] = jnp.where(low, near, far)
         sin_ref[g] = jnp.where(low, far, near)
 
-    def norm(x_ref, gain_ref, l):
-        total = jnp.zeros((ROWS, 1), F32)
+    def norm(x_ref, gain_ref, l, lo=0, n=ROWS):
+        rows = pl.ds(lo, n)
+        total = jnp.zeros((n, 1), F32)
         for j in range(NCH):
-            x = x_ref[j].astype(F32)
+            x = x_ref[j, rows].astype(F32)
             total = total + jnp.sum(x * x, axis=-1, keepdims=True)
         inv = lax.rsqrt(total * (1.0 / D) + 1e-5)
         for j in range(NCH):
             cols = pl.ds(j * CH, CH)
-            a_ref[:, cols] = (x_ref[j].astype(F32) * inv * gain_ref[l:l + 1, cols].astype(F32)).astype(BF16)
-
-    def rope(v, g):
-        swapped = jnp.where(first_half, pltpu.roll(v, 128 - HEAD // 2, 1), pltpu.roll(v, HEAD // 2, 1))
-        return v * cos_ref[g] + swapped * sin_ref[g]
-
-    def qkv(l, g):
-        k_new = jnp.dot(a_ref[...], wk_v[...], preferred_element_type=F32)
-        v_new = jnp.dot(a_ref[...], wv_v[...], preferred_element_type=F32).astype(BF16)
-        k_new = jnp.concatenate([rope(k_new[:, :128], g), rope(k_new[:, 128:], g)], axis=1).astype(BF16)
-        for i in range(2):
+            a_ref[rows, cols] = (x_ref[j, rows].astype(F32) * inv * gain_ref[l:l + 1, cols].astype(F32)).astype(BF16)
+
+    def rope(v, g, rows):
+        n = v.shape[0]
+        swapped = jnp.where(first_half[:n], pltpu.roll(v, 128 - HEAD // 2, 1), pltpu.roll(v, HEAD // 2, 1))
+        return v * cos_ref[g, rows] + swapped * sin_ref[g, rows]
+
+    def keys_values(l, g, lo=0, n=ROWS):
+        take = pl.ds(lo, n)
+        k_new = jnp.dot(a_ref[take], wk_v[...], preferred_element_type=F32)
+        v_new = jnp.dot(a_ref[take], wv_v[...], preferred_element_type=F32).astype(BF16)
+        k_new = jnp.concatenate([rope(k_new[:, :128], g, take), rope(k_new[:, 128:], g, take)], axis=1).astype(BF16)
+        parts = range(lo // SEG, (lo + n) // SEG)
+        for i in parts:
             rows = pl.ds(pl.multiple_of(segments(g, t, c)[i] * SEG, SEG), SEG)
-            kv[l, rows, 0:256] = k_new[i * SEG:(i + 1) * SEG]
-            kv[l, rows, 256:512] = v_new[i * SEG:(i + 1) * SEG]
-        for i in range(2):
+            kv[l, rows, 0:256] = k_new[i * SEG - lo:(i + 1) * SEG - lo]
+            kv[l, rows, 256:512] = v_new[i * SEG - lo:(i + 1) * SEG - lo]
+        for i in parts:
             for kind in ((1, 2, 0) if g == 0 else (1, 0)):
                 send_kv(l, kind, g, i, c, peers[kind]).start()
+
+    def queries(l, g, lo=0, n=ROWS):
+        take = pl.ds(lo, n)
         for h in range(4):
-            q = lax.dot_general(a_ref[...], slot[h * 256:(h + 1) * 256, :], (((1,), (1,)), ((), ())), preferred_element_type=F32)
+            q = lax.dot_general(a_ref[take], slot[h * 256:(h + 1) * 256, :], (((1,), (1,)), ((), ())), preferred_element_type=F32)
             for pair in range(2):
-                both = rope(q[:, pair * 128:(pair + 1) * 128], g)
+                both = rope(q[:, pair * 128:(pair + 1) * 128], g, take)
                 turned = pltpu.roll(both, HEAD, 1)
                 for odd in range(2):
                     value = both if odd == h % 2 else turned
-                    value = jnp.where(low if h % 2 == 0 else ~low, value, 0.0).astype(BF16)
-                    n = pair * 2 + odd
-                    for i in range(2):
-                        qh[g, i, h, n * SEG:(n + 1) * SEG, :] = value[i * SEG:(i + 1) * SEG]
+                    value = jnp.where(low[:n] if h % 2 == 0 else ~low[:n], value, 0.0).astype(BF16)
+                    m = pair * 2 + odd
+                    for i in range(lo // SEG, (lo + n) // SEG):
+                        qh[g, i, h, m * SEG:(m + 1) * SEG, :] = value[i * SEG - lo:(i + 1) * SEG - lo]
 
     def attention(l, g, parts=(0, 1)):
         for i in parts:
@@ -224,69 +243,90 @@
         norm(x_own, gain_attn, l)
         wait(load_kvw(l))
         wait(load_slot(wq.at[l]))
-        qkv(l, 0)
-        for j in range(NCH):
-            send_x(x_own.at[j], j).wait_recv()
-        norm(x_par, gain_attn, l)
-        qkv(l, 1)
-        start(load_slot(wo.at[l]))
-        if not last:
-            start(load_kvw(l + 1))
-        if last:
-            pass_wo(LATE[:1])
-        for i in range(2):
-            send_kv(l, 1, 1, i, across, across).wait_recv()
-            send_kv(l, 2, 1, i, across, beside).start()
-            if last and i == 0:
-                pass_wo(LATE[1:3])
+        keys_values(l, 0)
+        queries(l, 0)
 
         def wait_kv(i, l=l):
             for kind, g in ((0, 0), (1, 0), (2, 0), (0, 1), (2, 1)):
                 send_kv(l, kind, g, i, peers[kind], peers[kind]).wait_recv()
 
-        wait_kv(0)
+        def relay_kv(i, l=l):
+            send_kv(l, 1, 1, i, across, across).wait_recv()
+            send_kv(l, 2, 1, i, across, beside).start()
+
         if not last:
-            wait(load_slot(wo.at[l]))
+            for j in range(NCH):
+                send_tokens(0, j).wait_recv()
+            norm(x_par, gain_attn, l, 0, SEG)
+            keys_values(l, 1, 0, SEG)
+            queries(l, 1, 0, SEG)
+            relay_kv(0)
+            for j in range(NCH):
+                send_tokens(1, j).wait_recv()
+            norm(x_par, gain_attn, l, SEG, SEG)
+            keys_values(l, 1, SEG, SEG)
+            start(load_kvw(l + 1))
+            for j in range(NCH):
+                load_wo(j).wait()
+
+            def wo_chunk(lhs, j):
+                return jnp.dot(lhs, wd_v[lax.rem(j, RING), wo_rows(j)], preferred_element_type=F32)
+
             for i in range(2):
-                if i == 1:
-                    wait_kv(1)
+                wait_kv(i)
                 attention(l, 1, (i,))
 
                 def o_send(j, carry, i=i):
                     rows = pl.ds(i * SEG, SEG)
-                    sbuf[j, rows] = slot_chunk(o_ref[1, rows], j)
+                    sbuf[j, rows] = wo_chunk(o_ref[1, rows], j)
                     send_half(i, j).start()
                     return carry
                 lax.fori_loop(0, NCH, o_send, 0)
+                if i == 0:
+                    queries(l, 1, SEG, SEG)
+                    start(load_slot(wq.at[l + 1]))
+                    relay_kv(1)
             pass_wo(FIRST)
             attention(l, 0)
 
             def o_reduce(j, carry):
-                own = slot_chunk(o_ref[0], j)
+                own = wo_chunk(o_ref[0], j)
                 start(load_gu(0, j))
                 send_half(0, j).wait_recv()
                 send_half(1, j).wait_recv()
-                new = reduce_chunk(own, j)
-                send_x(x_own.at[j], j).wait_send()
-                x_own[j] = new
+                x_own[j] = reduce_chunk(own, j)
                 send_x(x_own.at[j], j).start()
                 return carry
             lax.fori_loop(0, NCH, o_reduce, 0)
             for p in MIDDLE:
                 send_wo(p).start()
+            for j in range(RING):
+                load_wd(0, j).start()
             relay_wo(FIRST)
-            start(load_slot(wq.at[l + 1]))
         else:
-            pass_wo(LATE[3:])
+            for j in range(NCH):
+                send_x(x_own.at[j], j).wait_recv()
+            norm(x_par, gain_attn, l)
+            keys_values(l, 1)
+            queries(l, 1)
+            start(load_slot(wo.at[l]))
+            pass_wo(LATE[:1])
+            relay_kv(0)
+            pass_wo(LATE[1:3])
+            relay_kv(1)
+            wait_kv(0)
+            pass_wo(LATE[3:4])
             attention(l, 0, (0,))
             send_o(0, 0).start()
+            pass_wo(LATE[4:5])
             wait_kv(1)
             attention(l, 0, (1,))
             send_o(0, 1).start()
-            relay_wo(LATE[:1])
+            pass_wo(LATE[5:6])
             attention(l, 1, (0,))
             send_o(1, 0).start()
-            relay_wo(LATE[1:])
+            pass_wo(LATE[6:])
+            relay_wo(LATE[:4])
             attention(l, 1, (1,))
             send_o(1, 1).start()
             wait(load_slot(wo.at[l]))
@@ -296,6 +336,7 @@
                 sbuf[j] = slot_chunk(o_ref[1], j)
                 return carry
             lax.fori_loop(0, NCH, o_near, 0)
+            relay_wo(LATE[4:])
             for p in range(PIECES):
                 spread_wo(0, p, beside, beside).wait_recv()
                 spread_wo(2, p, corner, beside).wait_recv()
@@ -401,6 +442,9 @@
             for i in range(2):
                 for kind in range(3):
                     send_kv(l, kind, g, i, c, beside).wait_send()
+    for i in range(2):
+        for j in range(NCH):
+            send_tokens(i, j).wait_send()
     for g in range(2):
         send_o(g, 0).wait_send()
         send_o(g, 1).wait_send()
@@ -459,8 +503,8 @@
                 pltpu.VMEM((2, ROWS, 128), F32),
                 pltpu.VMEM((2, ROWS, 128), F32),
                 pltpu.VMEM((2, ROWS, 128), F32),
-                dma((NCH,)), dma((NCH,)), dma((2,)), dma((2,)), dma((2, NGC)), dma((RING,)), dma((2, 2)),
-                dma((NCH,)), dma((NCH,)), dma((NCH,)), dma((NCH,)), dma((2, NCH)), dma((2, NCH)),
+                dma((NCH,)), dma((NCH,)), dma((2,)), dma((2,)), dma((2, NGC)), dma((RING,)), dma((NCH,)), dma((2, 2)),
+                dma((NCH,)), dma((NCH,)), dma((NCH,)), dma((NCH,)), dma((2, NCH)), dma((2, NCH)), dma((2, NCH)), dma((2, NCH)),
                 dma((LAYERS, 3, 2, 2)), dma((LAYERS, 3, 2, 2)), dma((2, 2)), dma((2, 2)),
                 dma((PIECES,)), dma((PIECES,)), dma((3, PIECES)), dma((3, PIECES)),
             ],

time: 158 us -> 155 us (0.981)
  Pallas kernels: 156 us -> 153 us
    pallas_call x1, Pallas kernels: 156 us -> 153 us  [body(): pl.pallas_call(kernel, out_shape=jax.ShapeDtypeStruct((ROWS, D), BF16), i...]
where the time goes in v6:
time: 155 us
  Pallas kernels  153 us (99%)
  local copies, waits for them, and re-layouts  1.88 us (1%)
    pallas_call x1, Pallas kernels, body(): pl.pallas_call(kernel, out_shape=jax.ShapeDtypeStruct((ROWS, D), BF16), i...  153 us

profile of v6, /device:TPU:0, one launch (start us, length us, event | category | flops | bytes accessed | tf_op | source)
XLA Modules:
  0.0 155.1 jit_solution(14333277012445804641)
XLA Ops:
  0.0 153.3 %decoder.1 = bf16[128,2048]{1,0:T(8,128)(2,1)} custom-call(bf16[128,2048]{1,0:T(8,128)(2,1)} %tokens.1, bf16[2,2048]{1,0:T(2,128)(2,1)} %gain_attn.1, bf16[2,2048]{1,0:T(2,128)(2,1)} %gain_mlp.1, f32[1024,128]{1,0:T(8,128)} %constant.2.clone.table, bf16[2,1024,2048]{2,1,0:T(8,128)(2,1)} %bitcast.4, bf16[2,2048,256]{2,1,0:T(8,128)(2,1)} %wk.1, ...), custom_call_target="tpu_custom_call" | custom-call | tf_op jit(solution)/shard_map/decoder/pallas_call | solution.py:480
  153.3 1.9 %copy.13 = bf16[128,2048]{1,0:T(8,128)(2,1)} copy(bf16[128,2048]{1,0:T(8,128)(2,1)} %decoder.1) | data formatting | bytes 1048576

commit v7 on v6

--- a/solution.py
+++ b/solution.py
@@ -13,7 +13,7 @@
 F32 = jnp.float32
 BF16 = jnp.bfloat16
 ROWS, SEG, D, HEAD, FF = 128, 64, 2048, 64, 4096
-CH, NCH = 256, 8
+CH, NCH, NTWO = 256, 8, 4
 GCH, NGC = 512, 8
 RING = 4
 PIECES, PIECE = 16, 16
@@ -57,12 +57,13 @@
         for copy in copies:
             copy.wait()
 
-    def send_x(src, j):
-        return pltpu.make_async_remote_copy(src, x_par.at[j], xs_sem.at[j], xr_sem.at[j], other, MESH)
-
-    def send_tokens(i, j):
-        rows, cols = pl.ds(i * SEG, SEG), pl.ds(j * CH, CH)
-        return pltpu.make_async_remote_copy(tokens.at[rows, cols], x_par.at[j, rows], ts_sem.at[i, j], tr_sem.at[i, j], other, MESH)
+    def send_x(k):
+        two = pl.ds(2 * k, 2)
+        return pltpu.make_async_remote_copy(x_own.at[two], x_par.at[two], xs_sem.at[k], xr_sem.at[k], other, MESH)
+
+    def send_tokens(i):
+        rows = pl.ds(i * SEG, SEG)
+        return pltpu.make_async_remote_copy(tokens.at[rows], act.at[1, rows, pl.ds(0, D)], ts_sem.at[i], tr_sem.at[i], other, MESH)
 
     def load_wo(j):
         cols = pl.ds(pl.multiple_of(j * CH, CH), CH)
@@ -71,16 +72,17 @@
     def wo_rows(j):
         return pl.ds(pl.multiple_of(j // RING * 1024, 1024), 1024)
 
-    def send_part(j):
-        return pltpu.make_async_remote_copy(sbuf.at[j], rbuf.at[j], ps_sem.at[j], pr_sem.at[j], other, MESH)
+    def send_part(k):
+        two = pl.ds(2 * k, 2)
+        return pltpu.make_async_remote_copy(sbuf.at[two], rbuf.at[two], ps_sem.at[k], pr_sem.at[k], other, MESH)
 
     def segments(g, ti, ci):
         k = (ti if g == 0 else 1 - ti) * 4 + ci
         return k, 15 - k
 
-    def send_half(i, j):
-        place = (j, pl.ds(i * SEG, SEG))
-        return pltpu.make_async_remote_copy(sbuf.at[place], rbuf.at[place], ds_sem.at[i, j], dr_sem.at[i, j], other, MESH)
+    def send_half(i, k):
+        place = (pl.ds(2 * k, 2), pl.ds(i * SEG, SEG))
+        return pltpu.make_async_remote_copy(sbuf.at[place], rbuf.at[place], ds_sem.at[i, k], dr_sem.at[i, k], other, MESH)
 
     def send_o(g, i):
         rows = pl.ds(i * SEG, SEG)
@@ -130,8 +132,7 @@
         pl.semaphore_signal(barrier, inc=1, device_id={'cp': to}, device_id_type=MESH)
     pl.semaphore_wait(barrier, 4)
     for i in range(2):
-        for j in range(NCH):
-            send_tokens(i, j).start()
+        send_tokens(i).start()
     for p in FIRST:
         send_wo(p).start()
     for j in range(NCH):
@@ -153,13 +154,17 @@
     def norm(x_ref, gain_ref, l, lo=0, n=ROWS):
         rows = pl.ds(lo, n)
         total = jnp.zeros((n, 1), F32)
+
+        def chunk(j):
+            return x_ref[1, rows, j * CH:(j + 1) * CH] if x_ref is act else x_ref[j, rows]
+
         for j in range(NCH):
-            x = x_ref[j, rows].astype(F32)
+            x = chunk(j).astype(F32)
             total = total + jnp.sum(x * x, axis=-1, keepdims=True)
         inv = lax.rsqrt(total * (1.0 / D) + 1e-5)
         for j in range(NCH):
             cols = pl.ds(j * CH, CH)
-            a_ref[rows, cols] = (x_ref[j, rows].astype(F32) * inv * gain_ref[l:l + 1, cols].astype(F32)).astype(BF16)
+            a_ref[rows, cols] = (chunk(j).astype(F32) * inv * gain_ref[l:l + 1, cols].astype(F32)).astype(BF16)
 
     def rope(v, g, rows):
         n = v.shape[0]
@@ -255,15 +260,13 @@
             send_kv(l, 2, 1, i, across, beside).start()
 
         if not last:
-            for j in range(NCH):
-                send_tokens(0, j).wait_recv()
-            norm(x_par, gain_attn, l, 0, SEG)
+            send_tokens(0).wait_recv()
+            norm(act, gain_attn, l, 0, SEG)
             keys_values(l, 1, 0, SEG)
             queries(l, 1, 0, SEG)
             relay_kv(0)
-            for j in range(NCH):
-                send_tokens(1, j).wait_recv()
-            norm(x_par, gain_attn, l, SEG, SEG)
+            send_tokens(1).wait_recv()
+            norm(act, gain_attn, l, SEG, SEG)
             keys_values(l, 1, SEG, SEG)
             start(load_kvw(l + 1))
             for j in range(NCH):
@@ -276,12 +279,13 @@
                 wait_kv(i)
                 attention(l, 1, (i,))
 
-                def o_send(j, carry, i=i):
+                def o_send(k, carry, i=i):
                     rows = pl.ds(i * SEG, SEG)
-                    sbuf[j, rows] = wo_chunk(o_ref[1, rows], j)
-                    send_half(i, j).start()
+                    for j in (2 * k, 2 * k + 1):
+                        sbuf[j, rows] = wo_chunk(o_ref[1, rows], j)
+                    send_half(i, k).start()
                     return carry
-                lax.fori_loop(0, NCH, o_send, 0)
+                lax.fori_loop(0, NTWO, o_send, 0)
                 if i == 0:
                     queries(l, 1, SEG, SEG)
                     start(load_slot(wq.at[l + 1]))
@@ -292,10 +296,16 @@
             def o_reduce(j, carry):
                 own = wo_chunk(o_ref[0], j)
                 start(load_gu(0, j))
-                send_half(0, j).wait_recv()
-                send_half(1, j).wait_recv()
+
+                @pl.when(lax.rem(j, 2) == 0)
+                def _():
+                    send_half(0, j // 2).wait_recv()
+                    send_half(1, j // 2).wait_recv()
                 x_own[j] = reduce_chunk(own, j)
-                send_x(x_own.at[j], j).start()
+
+                @pl.when(lax.rem(j, 2) == 1)
+                def _():
+                    send_x(j // 2).start()
                 return carry
             lax.fori_loop(0, NCH, o_reduce, 0)
             for p in MIDDLE:
@@ -304,8 +314,8 @@
                 load_wd(0, j).start()
             relay_wo(FIRST)
         else:
-            for j in range(NCH):
-                send_x(x_own.at[j], j).wait_recv()
+            for k in range(NTWO):
+                send_x(k).wait_recv()
             norm(x_par, gain_attn, l)
             keys_values(l, 1)
             queries(l, 1)
@@ -331,8 +341,10 @@
             send_o(1, 1).start()
             wait(load_slot(wo.at[l]))
 
+            for k in range(NTWO):
+                send_part(k).wait_send()
+
             def o_near(j, carry):
-                send_part(j).wait_send()
                 sbuf[j] = slot_chunk(o_ref[1], j)
                 return carry
             lax.fori_loop(0, NCH, o_near, 0)
@@ -357,8 +369,8 @@
         if not last:
             norm(x_own, gain_mlp, l)
             gate_up(0)
-            for j in range(NCH):
-                send_x(x_own.at[j], j).wait_recv()
+            for k in range(NTWO):
+                send_x(k).wait_recv()
             norm(x_par, gain_mlp, l)
             gate_up(1)
         else:
@@ -376,14 +388,18 @@
             load_wd(l, j).wait()
             return jnp.dot(act[g], wd_v[lax.rem(j, RING)], preferred_element_type=F32)
 
-        def down_send(j, carry, l=l, last=last):
-            part = down_chunk(1, j)
+        if not last:
+            for k in range(NTWO):
+                send_half(0, k).wait_send()
+                send_half(1, k).wait_send()
+
+        def down_send(j, carry, l=l):
+            sbuf[j] = down_chunk(1, j)
             load_wd(l, lax.rem(j + RING, NCH)).start()
-            if not last:
-                send_half(0, j).wait_send()
-                send_half(1, j).wait_send()
-            sbuf[j] = part
-            send_part(j).start()
+
+            @pl.when(lax.rem(j, 2) == 1)
+            def _():
+                send_part(j // 2).start()
             return carry
         lax.fori_loop(0, NCH, down_send, 0)
         if not last:
@@ -392,41 +408,43 @@
             recv_o(0, 0).wait_recv()
             recv_o(0, 1).wait_recv()
 
+            for k in range(NTWO):
+                send_x(k).wait_send()
+
             def o_own(j, carry):
-                new = (x_own[j].astype(F32) + (slot_chunk(o_ref[0], j) + far_chunk(0, j))).astype(BF16)
-                send_x(x_own.at[j], j).wait_send()
-                x_own[j] = new
+                x_own[j] = (x_own[j].astype(F32) + (slot_chunk(o_ref[0], j) + far_chunk(0, j))).astype(BF16)
                 return carry
             lax.fori_loop(0, NCH, o_own, 0)
             norm(x_own, gain_mlp, l)
             gate_up(0)
 
+        if not last:
+            for k in range(NTWO):
+                send_x(k).wait_send()
+
         def down_reduce(j, carry, l=l, last=last):
             own = down_chunk(0, j)
-            if last:
-                @pl.when(j < NCH - RING)
-                def _():
-                    load_wd(l, j + RING).start()
-            else:
-                @pl.when(j < NCH - RING)
-                def _():
-                    load_wd(l, j + RING).start()
-
+
+            @pl.when(j < NCH - RING)
+            def _():
+                load_wd(l, j + RING).start()
+            if not last:
                 @pl.when(j >= NCH - RING)
                 def _():
                     load_wd(l + 1, j + RING - NCH).start()
-            if not last:
                 start(load_gu(l + 1, j))
-            send_part(j).wait_recv()
-            new = reduce_chunk(own, j)
-            if not last:
-                send_x(x_own.at[j], j).wait_send()
-            x_own[j] = new
-            cols = pl.ds(pl.multiple_of(j * CH, CH), CH)
+
+            @pl.when(lax.rem(j, 2) == 0)
+            def _():
+                send_part(j // 2).wait_recv()
+            x_own[j] = reduce_chunk(own, j)
             if last:
+                cols = pl.ds(pl.multiple_of(j * CH, CH), CH)
                 pltpu.make_async_copy(x_own.at[j], out.at[:, cols], out_sem.at[j]).start()
             else:
-                send_x(x_own.at[j], j).start()
+                @pl.when(lax.rem(j, 2) == 1)
+                def _():
+                    send_x(j // 2).start()
             return carry
         lax.fori_loop(0, NCH, down_reduce, 0)
         if not last:
@@ -434,8 +452,9 @@
                 send_wo(p).start()
             relay_wo(MIDDLE)
 
+    for k in range(NTWO):
+        send_part(k).wait_send()
     for j in range(NCH):
-        send_part(j).wait_send()
         pltpu.make_async_copy(x_own.at[j], out.at[:, pl.ds(j * CH, CH)], out_sem.at[j]).wait()
     for l in range(LAYERS):
         for g in range(2):
@@ -443,8 +462,7 @@
                 for kind in range(3):
                     send_kv(l, kind, g, i, c, beside).wait_send()
     for i in range(2):
-        for j in range(NCH):
-            send_tokens(i, j).wait_send()
+        send_tokens(i).wait_send()
     for g in range(2):
         send_o(g, 0).wait_send()
         send_o(g, 1).wait_send()
@@ -504,7 +522,7 @@
                 pltpu.VMEM((2, ROWS, 128), F32),
                 pltpu.VMEM((2, ROWS, 128), F32),
                 dma((NCH,)), dma((NCH,)), dma((2,)), dma((2,)), dma((2, NGC)), dma((RING,)), dma((NCH,)), dma((2, 2)),
-                dma((NCH,)), dma((NCH,)), dma((NCH,)), dma((NCH,)), dma((2, NCH)), dma((2, NCH)), dma((2, NCH)), dma((2, NCH)),
+                dma((NTWO,)), dma((NTWO,)), dma((NTWO,)), dma((NTWO,)), dma((2, NTWO)), dma((2, NTWO)), dma((2,)), dma((2,)),
                 dma((LAYERS, 3, 2, 2)), dma((LAYERS, 3, 2, 2)), dma((2, 2)), dma((2, 2)),
                 dma((PIECES,)), dma((PIECES,)), dma((3, PIECES)), dma((3, PIECES)),
             ],

time: 155 us -> 156 us (level)
  no operation moved by 1% of the time
where the time goes in v7:
time: 156 us
  Pallas kernels  154 us (99%)
  local copies, waits for them, and re-layouts  1.88 us (1%)
    pallas_call x1, Pallas kernels, body(): pl.pallas_call(kernel, out_shape=jax.ShapeDtypeStruct((ROWS, D), BF16), i...  154 us

profile of v7, /device:TPU:0, one launch (start us, length us, event | category | flops | bytes accessed | tf_op | source)
XLA Modules:
  0.0 156.1 jit_solution(16684669318744029258)
XLA Ops:
  0.0 154.2 %decoder.1 = bf16[128,2048]{1,0:T(8,128)(2,1)} custom-call(bf16[128,2048]{1,0:T(8,128)(2,1)} %tokens.1, bf16[2,2048]{1,0:T(2,128)(2,1)} %gain_attn.1, bf16[2,2048]{1,0:T(2,128)(2,1)} %gain_mlp.1, f32[1024,128]{1,0:T(8,128)} %constant.2.clone.table, bf16[2,1024,2048]{2,1,0:T(8,128)(2,1)} %bitcast.4, bf16[2,2048,256]{2,1,0:T(8,128)(2,1)} %wk.1, ...), custom_call_target="tpu_custom_call" | custom-call | tf_op jit(solution)/shard_map/decoder/pallas_call | solution.py:498
  154.3 1.9 %copy.13 = bf16[128,2048]{1,0:T(8,128)(2,1)} copy(bf16[128,2048]{1,0:T(8,128)(2,1)} %decoder.1) | data formatting | bytes 1048576
